TPU v7x, 32 devices: a whole 2x2x4 slice. The times are simulated.
32 devices in a mesh: dp: 8 (over y, x, core), mp: 4 (over z).
Axes of the slice: x: 2, y: 2, z: 4, core: 2. Of those that a mesh axis runs over, the one named last changes fastest.
Arguments:
- grad_parts: bfloat16 [8, 4, 1024, 4096], P('dp', None, None, 'mp'), may hold values from -4000 to 4000
- master: float32 [4, 1024, 4096], P(None, 'dp', 'mp'), may hold values from -6 to 6
- first_moment: float32 [4, 1024, 4096], P(None, 'dp', 'mp'), may hold values from -4 to 4
- second_moment: float32 [4, 1024, 4096], P(None, 'dp', 'mp'), may hold values from 0.25 to 4
- left_basis: bfloat16 [4, 1024, 4096], P(None, 'dp', 'mp'), may hold values from -1 to 1, as said below
- right_basis: bfloat16 [4, 1024, 4096], P(None, 'dp', 'mp'), may hold values from -1 to 1, as said below
Outputs:
- weights: bfloat16 [4, 1024, 4096], P(None, None, 'mp')
- new_master: float32 [4, 1024, 4096], P(None, 'dp', 'mp')
- new_first: float32 [4, 1024, 4096], P(None, 'dp', 'mp')
- new_second: float32 [4, 1024, 4096], P(None, 'dp', 'mp')
Inputs may be any that keep to these rules, and one draw needn't show every extreme that they name: Each block left_basis[i, :, j * 1024 : (j + 1) * 1024] is an orthogonal 1024 x 1024 matrix up to rounding. Each block right_basis[i, :, j * 1024 : (j + 1) * 1024] is an orthogonal 1024 x 1024 matrix up to rounding.
All inputs are finite; a program needn't handle non-finite values.
Results may differ from a plain program's by a relative error of at most 0.02.
Values may be sent and summed in bfloat16 or wider, within the bound.
A program may use at most 128 MiB of HBM per device.

v0:
```python
import functools

import jax
import jax.numpy as jnp
from jax import lax
from jax.experimental import pallas as pl
from jax.experimental.pallas import tpu as pltpu
from jax.sharding import PartitionSpec as P

D = 4096
STEP = 10


beta_one = 0.95
beta_two = 0.95
epsilon = 1e-08
norm_epsilon = 1e-06
learning_rate = 0.3
decay_rate = 0.1

VMEM = pl.BlockSpec(memory_space=pltpu.VMEM)
MESH = pl.DeviceIdType.MESH


def remote(src, dst, send, recv, axis, index):
    return pltpu.make_async_remote_copy(
        src_ref=src,
        dst_ref=dst,
        send_sem=send,
        recv_sem=recv,
        device_id={axis: index},
        device_id_type=MESH,
    )


def enter(axes):
    barrier = pltpu.get_barrier_semaphore()
    total = 0
    for axis, size in axes:
        me = lax.axis_index(axis)
        for step in range(1, size):
            pl.semaphore_signal(
                barrier,
                inc=1,
                device_id={axis: lax.rem(me + step, size)},
                device_id_type=MESH,
            )
        total += size - 1
    pl.semaphore_wait(barrier, total)


class Gather:
    def __init__(self, n, nb, x, y, local, first, recv, second):
        self.n, self.nb, self.q = n, nb, n // nb
        self.x, self.y = x, y
        self.local, self.first, self.recv, self.second = local, first, recv, second
        self.me = lax.axis_index("dp")
        self.g, self.r = self.me // self.q, lax.rem(self.me, self.q)
        self.sent = []

    def go(self, src, slot, send, target):
        copy = remote(src, self.y.at[slot], send, self.recv.at[slot], "dp", target)
        copy.start()
        self.sent.append(copy)

    def arrived(self, slot):
        remote(
            self.y.at[slot], self.y.at[slot], self.first.at[0], self.recv.at[slot], "dp", self.me
        ).wait_recv()

    def start(self):
        nb, q, me, g, r = self.nb, self.q, self.me, self.g, self.r
        for j in range(1, nb):
            other = lax.rem(g + j, nb)
            self.go(self.x.at[other], me, self.first.at[j], other * q + r)
        for p in range(1, q):
            self.go(self.x.at[g], me, self.second.at[p], g * q + lax.rem(r + p, q))
        self.own = pltpu.make_async_copy(self.x.at[g], self.y.at[me], self.local.at[0])
        self.own.start()

    def forward(self):
        nb, q, g, r = self.nb, self.q, self.g, self.r
        for j in range(1, nb):
            slot = lax.rem(g + nb - j, nb) * q + r
            self.arrived(slot)
            for p in range(1, q):
                self.go(
                    self.y.at[slot], slot, self.second.at[j * q + p], g * q + lax.rem(r + p, q)
                )

    def finish(self):
        nb, q, r = self.nb, self.q, self.r
        self.own.wait()
        for p in range(1, q):
            for j in range(nb):
                self.arrived(j * q + lax.rem(r + p, q))
        for copy in self.sent:
            copy.wait_send()

    @staticmethod
    def scratch(n, nb):
        return [
            pltpu.SemaphoreType.DMA((1,)),
            pltpu.SemaphoreType.DMA((nb,)),
            pltpu.SemaphoreType.DMA((n,)),
            pltpu.SemaphoreType.DMA((n,)),
        ]


class Exchange:
    def __init__(self, n, nb, to_rows, x, y, local, send, recv):
        q = n // nb
        me = lax.axis_index("dp")
        self.nb, self.x, self.y = nb, x, y
        self.local, self.send, self.recv, self.me = local, send, recv, me
        owner = lax.rem(me, q) * nb
        first = me // nb
        if to_rows:
            self.targets = [owner + k for k in range(nb)]
            self.slot = me // q
            self.sources = [k * q + first for k in range(nb)]
        else:
            self.targets = [k * q + first for k in range(nb)]
            self.slot = lax.rem(me, nb)
            self.sources = [owner + k for k in range(nb)]

    def copy(self, k):
        return remote(
            self.x.at[k],
            self.y.at[self.slot],
            self.send.at[k],
            self.recv.at[self.slot],
            "dp",
            self.targets[k],
        )

    def mine(self, k):
        return pltpu.make_async_copy(self.x.at[k], self.y.at[self.slot], self.local.at[0])

    def start(self):
        for k in range(self.nb):

            @pl.when(self.targets[k] != self.me)
            def _():
                self.copy(k).start()

            @pl.when(self.targets[k] == self.me)
            def _():
                self.mine(k).start()

    def finish(self):
        for k in range(self.nb):

            @pl.when(self.sources[k] != self.me)
            def _():
                remote(
                    self.y.at[k], self.y.at[k], self.send.at[k], self.recv.at[k], "dp", self.me
                ).wait_recv()

            @pl.when(self.targets[k] != self.me)
            def _():
                self.copy(k).wait_send()

            @pl.when(self.targets[k] == self.me)
            def _():
                self.mine(k).wait()

    @staticmethod
    def scratch(nb):
        return [
            pltpu.SemaphoreType.DMA((1,)),
            pltpu.SemaphoreType.DMA((nb,)),
            pltpu.SemaphoreType.DMA((nb,)),
        ]


class Share:
    def __init__(self, axis, size, x, y, local, send, recv):
        self.axis, self.size, self.x, self.y = axis, size, x, y
        self.local, self.send, self.recv = local, send, recv
        self.me = lax.axis_index(axis)

    def copy(self, j):
        return remote(
            self.x,
            self.y.at[self.me],
            self.send.at[j],
            self.recv.at[self.me],
            self.axis,
            lax.rem(self.me + j, self.size),
        )

    def start(self):
        for j in range(1, self.size):
            self.copy(j).start()
        self.own = pltpu.make_async_copy(self.x, self.y.at[self.me], self.local.at[0])
        self.own.start()

    def finish(self):
        self.own.wait()
        for j in range(1, self.size):
            slot = lax.rem(self.me + j, self.size)
            remote(
                self.y.at[slot], self.y.at[slot], self.send.at[j], self.recv.at[slot], self.axis, slot
            ).wait_recv()
        for j in range(1, self.size):
            self.copy(j).wait_send()

    @staticmethod
    def scratch(size):
        return [
            pltpu.SemaphoreType.DMA((1,)),
            pltpu.SemaphoreType.DMA((size,)),
            pltpu.SemaphoreType.DMA((size,)),
        ]


def bases_kernel(n, nb, left, right, master, left_out, right_out, master_out, *sems):
    enter([("dp", n)])
    one = Gather(n, nb, right, right_out, *sems[0:4])
    two = Gather(n, nb, left, left_out, *sems[4:8])
    three = Exchange(n, nb, False, master, master_out, *sems[8:11])
    one.start()
    two.start()
    three.start()
    one.forward()
    two.forward()
    one.finish()
    two.finish()
    three.finish()


def gather_kernel(n, nb, x, y, *sems):
    enter([("dp", n)])
    one = Gather(n, nb, x, y, *sems)
    one.start()
    one.forward()
    one.finish()


def scatter_kernel(n, nb, x, y, *sems):
    enter([("dp", n)])
    one = Exchange(n, nb, True, x, y, *sems)
    one.start()
    one.finish()


def scatter_sum_kernel(n, m, nb, x, part, y, parts, *sems):
    enter([("dp", n), ("mp", m)])
    two = Share("mp", m, part, parts, *sems[3:6])
    two.start()
    one = Exchange(n, nb, True, x, y, *sems[0:3])
    one.start()
    two.finish()
    one.finish()


def group_kernel(n, nb, x, part, y, parts, *sems):
    enter([("dp", n)])
    q = n // nb
    me = lax.axis_index("dp")
    g, r = me // q, lax.rem(me, q)
    local, send, recv = sems[0:3]
    copies = []
    for p in range(1, q):
        copy = remote(
            x, y.at[r], send.at[p], recv.at[r], "dp", g * q + lax.rem(r + p, q)
        )
        copy.start()
        copies.append(copy)
    two = Share("dp", n, part, parts, *sems[3:6])
    two.start()
    own = pltpu.make_async_copy(x, y.at[r], local.at[0])
    own.start()
    own.wait()
    for p in range(1, q):
        slot = lax.rem(r + p, q)
        remote(y.at[slot], y.at[slot], send.at[p], recv.at[slot], "dp", me).wait_recv()
    two.finish()
    for copy in copies:
        copy.wait_send()


def call(kernel, shapes, scratch, collective_id, *args):
    moved = sum(s.size * s.dtype.itemsize for s in shapes)
    return pl.pallas_call(
        kernel,
        out_shape=shapes,
        in_specs=[VMEM] * len(args),
        out_specs=[VMEM] * len(shapes),
        scratch_shapes=scratch,
        compiler_params=pltpu.CompilerParams(
            collective_id=collective_id, has_side_effects=True, vmem_limit_bytes=32 * 1024 * 1024
        ),
        cost_estimate=pl.CostEstimate(flops=0, bytes_accessed=16 * moved, transcendentals=0),
    )(*args)


def per_device(n, m, grad_parts, master, first_moment, second_moment, left_basis, right_basis):
    bf16, f32 = jnp.bfloat16, jnp.float32
    nb, rb, cols = master.shape
    blk = rb * n
    q = n // nb
    hb = blk // q
    r = lax.rem(lax.axis_index("dp"), q)
    pieces = jax.ShapeDtypeStruct((nb, rb, cols), bf16)
    block = jax.ShapeDtypeStruct((n, rb, cols), bf16)
    low_sum = lax.psum_scatter(
        grad_parts.reshape(nb * blk, cols), "dp", scatter_dimension=0, tiled=True
    )
    left, right, master_low = call(
        functools.partial(bases_kernel, n, nb),
        [block, block, pieces],
        Gather.scratch(n, nb) * 2 + Exchange.scratch(nb),
        0,
        left_basis,
        right_basis,
        master.astype(bf16),
    )
    left, right = left.reshape(blk, cols), right.reshape(blk, cols)
    left_cols = lax.dynamic_slice_in_dim(left, r * hb, hb, axis=1)
    left_rows = lax.dynamic_slice_in_dim(left, r * hb, hb, axis=0)
    gradient = low_sum.astype(f32)
    part = jnp.full((8, 128), jnp.sum(gradient * gradient), f32)
    grad_block, parts = call(
        functools.partial(group_kernel, n, nb),
        [
            jax.ShapeDtypeStruct((q, hb, cols), bf16),
            jax.ShapeDtypeStruct((n, 8, 128), f32),
        ],
        Share.scratch(q) + Share.scratch(n),
        1,
        low_sum,
        part,
    )
    part = jnp.sum(parts, axis=0)
    turned = jnp.dot(
        grad_block.reshape(blk, cols), right, preferred_element_type=f32
    ).astype(bf16)
    rotated_rows = lax.dot_general(
        left_cols, turned, (((0,), (0,)), ((), ())), preferred_element_type=f32
    ).astype(bf16)
    rotated, parts = call(
        functools.partial(scatter_sum_kernel, n, m, nb),
        [pieces, jax.ShapeDtypeStruct((m, 8, 128), f32)],
        Exchange.scratch(nb) + Share.scratch(m),
        2,
        rotated_rows.reshape(nb, rb, cols),
        part,
    )
    squares_sum = jnp.sum(parts[:, 0, 0])
    clip_scale = jnp.minimum(1.0, 2.0 * D / jnp.sqrt(squares_sum + norm_epsilon))
    clipped = clip_scale * rotated.astype(f32)
    new_first = beta_one * first_moment + (1.0 - beta_one) * clipped
    new_second = beta_two * second_moment + (1.0 - beta_two) * clipped * clipped
    bias_one = 1.0 - beta_one**STEP
    bias_two = 1.0 - beta_two**STEP
    direction = (new_first / bias_one / (jnp.sqrt(new_second / bias_two) + epsilon)).astype(bf16)
    (direction_block,) = call(
        functools.partial(gather_kernel, n, nb), [block], Gather.scratch(n, nb), 3, direction
    )
    back = lax.dot_general(
        direction_block.reshape(blk, cols),
        right,
        (((1,), (1,)), ((), ())),
        preferred_element_type=f32,
    ).astype(bf16)
    update = jnp.dot(left_rows, back, preferred_element_type=f32)
    keep = 1.0 - learning_rate * decay_rate
    weight_rows = (
        master_low.reshape(hb, cols).astype(f32) * keep - learning_rate * update
    ).astype(bf16)
    weights = lax.all_gather(weight_rows, "dp", axis=0, tiled=True).reshape(nb, blk, cols)
    (update_rows,) = call(
        functools.partial(scatter_kernel, n, nb),
        [pieces],
        Exchange.scratch(nb),
        4,
        update.astype(bf16).reshape(nb, rb, cols),
    )
    new_master = master * keep - learning_rate * update_rows.astype(f32)
    return (weights, new_master, new_first, new_second)


def solution(mesh):
    n, m = mesh.shape["dp"], mesh.shape["mp"]
    return jax.shard_map(
        functools.partial(per_device, n, m),
        mesh=mesh,
        in_specs=(
            P("dp", None, None, "mp"),
            P(None, "dp", "mp"),
            P(None, "dp", "mp"),
            P(None, "dp", "mp"),
            P(None, "dp", "mp"),
            P(None, "dp", "mp"),
        ),
        out_specs=(
            P(None, None, "mp"),
            P(None, "dp", "mp"),
            P(None, "dp", "mp"),
            P(None, "dp", "mp"),
        ),
        check_vma=False,
    )
```

profile of v0, /device:TPU:0, one launch (start us, length us, event | category | flops | bytes accessed | tf_op | source)
XLA Modules:
  0.0 228.5 jit_solution(6726912487059157967)
XLA Ops:
  7.2 0.0 reduce-scatter.2.cloned.1.call-start
  7.2 0.7 reduce-scatter.2.cloned.1.call-update
  7.9 0.0 copy-start.1
  7.9 0.0 copy-start.2
  7.9 0.0 all-gather.2.cloned.1.call-start
  8.0 1.9 convert_element_type.34.master
  9.9 0.0 copy-done.1
  9.9 0.2 copy-done.2
  10.1 48.1 %shard_map.93 = (bf16[8,128,1024]{2,1,0:T(8,128)(2,1)S(1)}, bf16[8,128,1024]{2,1,0:T(8,128)(2,1)S(1)}, bf16[4,128,1024]{2,1,0:T(8,128)(2,1)S(1)}) custom-call(bf16[4,128,1024]{2,1,0:T(8,128)(2,1)S(1)} %copy-done.1, bf16[4,128,1024]{2,1,0:T(8,128)(2,1)S(1)} %copy-done.2, bf16[4,128,1024]{2,1,0:T(8,128)(2,1)S(1)} %convert_element_type.34.master), custom_call_target="tpu_custom_call" | custom-call | bytes 83886080 | tf_op jit(solution)/shard_map/pallas_call | solution.py:286
  58.1 0.0 copy-start.3
  58.2 1.3 copy-done.3
  59.5 0.0 copy-start.4
  59.5 1.3 copy-done.4
  60.8 1.6 convert_multiply_fusion.1
  62.4 31.3 %reduce-scatter.2.cloned.1.call-done.x = bf16[512,1024]{1,0:T(8,128)(2,1)} async-done(((bf16[4096,1024]{1,0:T(8,128)(2,1)}), bf16[512,1024]{1,0:T(8,128)(2,1)}) %reduce-scatter.2.cloned.1.call-update) | async-done | bytes 1048592 | tf_op jit(solution)/shard_map/reduce_scatter | solution.py:308
  93.7 2.4 %multiply_reduce_fusion = f32[]{:T(128)} fusion(bf16[512,1024]{1,0:T(8,128)(2,1)} %reduce-scatter.2.cloned.1.call-done.x), kind=kLoop, calls=%fused_computation.12 | loop fusion | flops 1572863 | bytes 1048580 | tf_op jit(solution)/shard_map/reduce_sum | solution.py:324
  96.1 0.6 broadcast_in_dim.3.part
  96.7 0.0 copy-start
  96.7 1.2 copy-done
  97.9 4.8 %shard_map.94 = (bf16[2,512,1024]{2,1,0:T(8,128)(2,1)S(1)}, f32[8,8,128]{2,1,0:T(8,128)S(1)}) custom-call(bf16[512,1024]{1,0:T(8,128)(2,1)S(1)} %copy-done, f32[8,128]{1,0:T(8,128)S(1)} %broadcast_in_dim.3.part), custom_call_target="tpu_custom_call" | custom-call | bytes 34078720 | tf_op jit(solution)/shard_map/pallas_call | solution.py:286
  102.7 0.0 copy-start.5
  102.8 1.3 copy-done.5
  104.1 5.9 %fusion.6 = bf16[512,1024]{1,0:T(8,128)(2,1)S(1)} fusion(bf16[1024,1024]{1,0:T(8,128)(2,1)} %bitcast.23, bf16[1024,1024]{1,0:T(8,128)(2,1)} %bitcast.21, bf16[1024,1024]{1,0:T(8,128)(2,1)} %bitcast.19, s32[]{:T(128)S(6)} %select_n.4), kind=kOutput, calls=%fused_computation.14 | convolution fusion | flops 3222798336 | bytes 6291460 | tf_op jit(solution)/shard_map/dot_general | solution.py:340
  110.0 15.1 %shard_map.95 = (bf16[4,128,1024]{2,1,0:T(8,128)(2,1)S(1)}, f32[4,8,128]{2,1,0:T(8,128)S(1)}) custom-call(bf16[4,128,1024]{2,1,0:T(8,128)(2,1)S(1)} %bitcast.18, f32[8,128]{1,0:T(8,128)S(1)} %reduce_sum.28.part), custom_call_target="tpu_custom_call" | custom-call | bytes 17039360 | tf_op jit(solution)/shard_map/pallas_call | solution.py:286
  125.1 0.6 slice_reduce_fusion
  126.4 5.7 %divide_convert_fusion = (bf16[4,128,1024]{2,1,0:T(8,128)(2,1)S(1)}, f32[4,128,1024]{2,1,0:T(8,128)}, f32[4,128,1024]{2,1,0:T(8,128)}) fusion(bf16[4,128,1024]{2,1,0:T(8,128)(2,1)S(1)} %get-tuple-element.17, f32[]{:T(128)S(6)} %min_shard_map.3, f32[4,128,1024]{2,1,0:T(8,128)} %param.8, f32[4,128,1024]{2,1,0:T(8,128)} %param.9), kind=kLoop, calls=%fused_computation.8 | loop fusion | flops 6815744 | bytes 10485764 | tf_op jit(solution)/shard_map/convert_element_type | solution.py:358
  132.1 18.2 %shard_map.96 = bf16[8,128,1024]{2,1,0:T(8,128)(2,1)S(1)} custom-call(bf16[4,128,1024]{2,1,0:T(8,128)(2,1)S(1)} %get-tuple-element.18.x), custom_call_target="tpu_custom_call" | custom-call | bytes 33554432 | tf_op jit(solution)/shard_map/pallas_call | solution.py:286
  150.3 7.1 %fusion.18 = (bf16[512,1024]{1,0:T(8,128)(2,1)S(1)}, bf16[512,1024]{1,0:T(8,128)(2,1)}) fusion(f32[4,128,1024]{2,1,0:T(8,128)} %convert_multiply_fusion.1, bf16[1024,1024]{1,0:T(8,128)(2,1)S(1)} %bitcast.16, bf16[1024,1024]{1,0:T(8,128)(2,1)} %bitcast.22, bf16[1024,1024]{1,0:T(8,128)(2,1)} %bitcast.20, s32[]{:T(128)S(6)} %select_n.4), kind=kOutput, calls=%fused_computation.22 | convolution fusion | flops 3224371200 | bytes 9437188 | tf_op jit(solution)/shard_map/dot_general | solution.py:368
  157.3 0.0 copy-start.6
  157.4 0.0 all-gather.2.cloned.1.call-update
  157.4 20.0 %shard_map.97 = bf16[4,128,1024]{2,1,0:T(8,128)(2,1)S(1)} custom-call(bf16[4,128,1024]{2,1,0:T(8,128)(2,1)S(1)} %bitcast.17), custom_call_target="tpu_custom_call" | custom-call | bytes 16777216 | tf_op jit(solution)/shard_map/pallas_call | solution.py:286
  177.4 0.0 copy-done.6
  177.4 1.7 multiply_subtract_fusion
  179.1 34.9 %all-gather.2.cloned.1.call-done = bf16[4096,1024]{1,0:T(8,128)(2,1)} async-done(((bf16[512,1024]{1,0:T(8,128)(2,1)}), bf16[4096,1024]{1,0:T(8,128)(2,1)}) %all-gather.2.cloned.1.call-update) | async-done | bytes 8388624 | tf_op jit(solution)/shard_map/all_gather | solution.py:373
  213.9 7.8 %copy.11 = bf16[4,1024,1024]{2,1,0:T(8,128)(2,1)} copy(bf16[4,1024,1024]{2,1,0:T(8,128)(2,1)} %bitcast.25) | data formatting | bytes 16777216
  (1 shorter events, 0.0 us)
Async XLA Ops:
  7.2 86.5 %reduce-scatter.2.cloned.1.call-start = ((), (), s32[]{:S(2)}) async-start(), calls=%async_computation.1 | async-start | bytes 9437184 | tf_op jit(solution)/shard_map/reduce_scatter | solution.py:308
  7.9 2.0 copy-start.1
  7.9 2.2 copy-start.2
  7.9 206.0 %all-gather.2.cloned.1.call-start = ((), (), s32[]{:S(2)}) async-start(), calls=%async_computation.2 | async-start | bytes 9437184 | tf_op jit(solution)/shard_map/all_gather | solution.py:373
  58.1 1.4 copy-start.3
  59.5 1.3 copy-start.4
  96.7 1.2 copy-start
  102.7 1.3 copy-start.5
  157.3 20.0 %copy-start.6 = (f32[4,128,1024]{2,1,0:T(8,128)S(1)}, f32[4,128,1024]{2,1,0:T(8,128)}, u32[]{:S(2)}) copy-start(f32[4,128,1024]{2,1,0:T(8,128)} %param.7) | copy-start | bytes 6291460
Sparse Core Ops, SparseCore 0:
  11.4 82.2 reduce-scatter.1
  157.5 56.3 all-gather.1
where the time goes:
time: 229 us
  Pallas kernels  106 us (46%)
  waiting for transfers between devices  66.8 us (29%)
  between operations  14.9 us (7%)
  other arithmetic  13.9 us (6%)
  local copies, waits for them, and re-layouts  13.8 us (6%)
  matrix products  13 us (6%)
    pallas_call x5, Pallas kernels, call(): pl.pallas_call(kernel, out_shape=shapes, in_specs=[VMEM] * len(args), out...  106 us
    all_gather x1, waiting for transfers between devices, per_device(): lax.all_gather(weight_rows, 'dp', axis=0, tiled=True).reshape(nb, blk, cols)  34.9 us
    reduce_scatter x1, waiting for transfers between devices, per_device(): lax.psum_scatter(grad_parts.reshape(nb * blk, cols), 'dp', scatter_dimens...  31.3 us
    unnamed x15, local copies, waits for them, and re-layouts  13.2 us
    dot_general x1, matrix products, per_device(): update = jnp.dot(left_rows, back, preferred_element_type=f32)  7.06 us
    dot_general x1, matrix products, per_device(): lax.dot_general(left_cols, turned, (((0,), (0,)), ((), ())), preferred_el...  5.95 us
    convert_element_type x1, other arithmetic, per_device(): (new_first / bias_one / (jnp.sqrt(new_second / bias_two) + epsilon)).asty...  5.73 us
  transfers between devices with their start and end apart: 2, of which 2 were waited for; matrix products, arithmetic and copies ran while one was open for 2% of the time, Pallas kernels for 30%

commit v1 on v0

--- a/solution.py
+++ b/solution.py
@@ -296,7 +296,7 @@
     )(*args)
 
 
-def per_device(n, m, grad_parts, master, first_moment, second_moment, left_basis, right_basis):
+def per_device_general(n, m, grad_parts, master, first_moment, second_moment, left_basis, right_basis):
     bf16, f32 = jnp.bfloat16, jnp.float32
     nb, rb, cols = master.shape
     blk = rb * n
@@ -382,6 +382,503 @@
     return (weights, new_master, new_first, new_second)
 
 
+SEMAPHORES = (
+    ("local", 5),
+    ("grad", 4),
+    ("pair_s", 4),
+    ("pair_r", 4),
+    ("right_s", 8),
+    ("right_r", 8),
+    ("left_s", 8),
+    ("left_r", 8),
+    ("one_s", 8),
+    ("one_r", 8),
+    ("two_s", 4),
+    ("two_r", 4),
+    ("turned_s", 4),
+    ("turned_r", 4),
+    ("rot_s", 4),
+    ("rot_r", 4),
+    ("dir_s", 4),
+    ("dir_r", 4),
+    ("back_s", 4),
+    ("back_r", 4),
+    ("low_s", 4),
+    ("low_r", 4),
+    ("out_s", 12),
+    ("pass_s", 16),
+    ("out_r", 32),
+    ("norm_s", 8),
+    ("norm_r", 8),
+    ("mesh_s", 8),
+    ("mesh_r", 8),
+)
+
+
+def step_kernel(
+    n,
+    m,
+    grad,
+    master,
+    first,
+    second,
+    left_in,
+    right_in,
+    weights,
+    new_master,
+    new_first,
+    new_second,
+    acc,
+    pair_recv,
+    left,
+    right,
+    left_t,
+    hop_one,
+    hop_two,
+    turned,
+    rot_send,
+    rot_recv,
+    dir_send,
+    dir_recv,
+    back,
+    low_send,
+    low_recv,
+    squares,
+    part,
+    parts_dp,
+    total,
+    parts_mp,
+    *sem_refs,
+):
+    sem = {name: ref for (name, _), ref in zip(SEMAPHORES, sem_refs)}
+    f32, bf16 = jnp.float32, jnp.bfloat16
+    nb, rb, cols = master.shape
+    half = nb * rb
+    wide = cols // 2
+    me = lax.axis_index("dp")
+    c, k = me // 2, lax.rem(me, 2)
+    cy, cx = c // 2, lax.rem(c, 2)
+    xn, yn = 2 * cy + (1 - cx), 2 * (1 - cy) + cx
+    one, two = (1 - k) * xn + k * yn, k * xn + (1 - k) * yn
+    partner = me + 1 - 2 * k
+    swapped = (0, 2, 1, 3)
+    keep = 1.0 - learning_rate * decay_rate
+
+    def chip(i):
+        return c + (1 - i // 2) * (one - c) + (1 - i % 2) * (two - c)
+
+    def device(i):
+        return 2 * chip(i) + k
+
+    def rows(s):
+        return pl.ds(pl.multiple_of(s * rb, rb), rb)
+
+    def send(src, dst, send_sem, recv_sem, target):
+        remote(src, dst, send_sem, recv_sem, "dp", target).start()
+
+    def received(ref, recv_sem):
+        remote(ref, ref, recv_sem, recv_sem, "dp", me).wait_recv()
+
+    def sent(ref, send_sem):
+        remote(ref, ref, send_sem, send_sem, "dp", me).wait_send()
+
+    def strips(body, step=32):
+        @pl.loop(0, rb // step)
+        def _(t):
+            body(lambda base: pl.ds(pl.multiple_of(base + t * step, step), step))
+
+    enter([("dp", n), ("mp", m)])
+
+    bases = ((right_in, right, "right", 0), (left_in, left, "left", 1))
+    locals_in = []
+
+    def fetch(src, dst, local_sem):
+        copy = pltpu.make_async_copy(src, dst, local_sem)
+        copy.start()
+        locals_in.append(copy)
+
+    for x_in, x, name, _ in bases:
+        for i in range(3):
+            send(
+                x_in.at[chip(i)],
+                x.at[rows(me)],
+                sem[name + "_s"].at[i],
+                sem[name + "_r"].at[me],
+                device(i),
+            )
+    for i in range(nb):
+        b = chip(i)
+        send(
+            grad.at[b, pl.ds((1 - k) * half, half)],
+            pair_recv.at[i],
+            sem["pair_s"].at[i],
+            sem["pair_r"].at[i],
+            partner,
+        )
+        fetch(grad.at[b, pl.ds(k * half, half)], acc.at[i], sem["grad"].at[i])
+    for x_in, x, name, slot in bases:
+        send(x_in.at[c], x.at[rows(me)], sem[name + "_s"].at[3], sem[name + "_r"].at[me], partner)
+        fetch(x_in.at[c], x.at[rows(me)], sem["local"].at[slot])
+    fetch(master, new_master, sem["local"].at[2])
+    fetch(first, new_first, sem["local"].at[3])
+    fetch(second, new_second, sem["local"].at[4])
+
+    for i in range(nb):
+        j = swapped[i]
+        locals_in[i].wait()
+        received(pair_recv.at[j], sem["pair_r"].at[j])
+
+        @pl.loop(0, nb)
+        def _(q):
+            def add(at):
+                r = at(q * rb)
+                acc[i, r] = (acc[i, r].astype(f32) + pair_recv[j, r].astype(f32)).astype(bf16)
+
+            strips(add)
+            if i < 2:
+                send(
+                    acc.at[i, rows(q)],
+                    hop_one.at[i, rows(q)],
+                    sem["one_s"].at[i * nb + q],
+                    sem["one_r"].at[i * nb + q],
+                    2 * one + k,
+                )
+
+    locals_in[6].wait()
+
+    @pl.loop(0, nb)
+    def _(b):
+        def narrow(at):
+            low_send[b, at(0)] = new_master[b, at(0)].astype(bf16)
+
+        strips(narrow)
+
+    def own_low(at):
+        low_recv[c, at(0)] = new_master[c, at(0)].astype(bf16)
+
+    strips(own_low)
+
+    def send_low(i):
+        send(
+            low_send.at[chip(i)], low_recv.at[c], sem["low_s"].at[i], sem["low_r"].at[c], device(i)
+        )
+
+    for _, x, name, slot in bases:
+        for i in range(3):
+            s = device(i)
+            received(x.at[rows(s)], sem[name + "_r"].at[s])
+            send(
+                x.at[rows(s)],
+                x.at[rows(s)],
+                sem[name + "_s"].at[4 + i],
+                sem[name + "_r"].at[s],
+                partner,
+            )
+
+    @pl.loop(0, nb)
+    def _(q):
+        received(hop_one.at[0, rows(q)], sem["one_r"].at[q])
+
+        def add(at):
+            r = at(q * rb)
+            acc[2, r] = (acc[2, r].astype(f32) + hop_one[0, r].astype(f32)).astype(bf16)
+
+        strips(add)
+        send(
+            acc.at[2, rows(q)],
+            hop_two.at[rows(q)],
+            sem["two_s"].at[q],
+            sem["two_r"].at[q],
+            2 * two + k,
+        )
+
+    send_low(0)
+    for _, x, name, slot in bases:
+        locals_in[4 + slot].wait()
+        for i in range(4):
+            s = 2 * chip(i) + 1 - k
+            received(x.at[rows(s)], sem[name + "_r"].at[s])
+
+    @pl.loop(0, nb)
+    def _(i):
+        left_t[i] = left[:, rows(device(i))].T
+
+    squares[...] = jnp.zeros_like(squares)
+
+    @pl.loop(0, nb)
+    def _(q):
+        received(hop_two.at[rows(q)], sem["two_r"].at[q])
+        received(hop_one.at[1, rows(q)], sem["one_r"].at[nb + q])
+
+        def add(at):
+            r = at(q * rb)
+            g = acc[3, r].astype(f32) + hop_one[1, r].astype(f32) + hop_two[r].astype(f32)
+            acc[3, r] = g.astype(bf16)
+            squares[...] += jnp.sum((g * g).reshape(-1, 8, cols), axis=0)
+
+        strips(add)
+
+        @pl.when(q == nb - 1)
+        def _():
+            folded = squares[:, 0:128]
+            for t in range(1, cols // 128):
+                folded = folded + squares[:, t * 128 : (t + 1) * 128]
+            part[...] = folded
+            for j in range(1, n):
+                send(
+                    part,
+                    parts_dp.at[me],
+                    sem["norm_s"].at[j],
+                    sem["norm_r"].at[me],
+                    lax.rem(me + j, n),
+                )
+
+        s = k * nb + q
+        for t in range(2):
+            at = pl.ds(t * wide, wide)
+            turned[rows(s), at] = jnp.dot(
+                acc[3, rows(q)], right[:, at], preferred_element_type=f32
+            ).astype(bf16)
+        send(
+            turned.at[rows(s)],
+            turned.at[rows(s)],
+            sem["turned_s"].at[q],
+            sem["turned_r"].at[q],
+            partner,
+        )
+
+    for q in range(nb):
+        received(turned.at[rows((1 - k) * nb + q)], sem["turned_r"].at[q])
+
+    @pl.loop(0, nb)
+    def _(i):
+        for t in range(2):
+            at = pl.ds(t * wide, wide)
+            rot_send[i, :, at] = jnp.dot(
+                left_t[i], turned[:, at], preferred_element_type=f32
+            ).astype(bf16)
+
+        @pl.when(i < 3)
+        def _():
+            send(
+                rot_send.at[i], rot_recv.at[i], sem["rot_s"].at[i], sem["rot_r"].at[i], device(i)
+            )
+
+    send_low(1)
+
+    folded = part[...]
+    for j in range(1, n):
+        s = lax.rem(me + j, n)
+        received(parts_dp.at[s], sem["norm_r"].at[s])
+        folded = folded + parts_dp[s]
+    total[...] = folded
+    z = lax.axis_index("mp")
+    for j in range(1, m):
+        remote(
+            total,
+            parts_mp.at[z],
+            sem["mesh_s"].at[j],
+            sem["mesh_r"].at[z],
+            "mp",
+            lax.rem(z + j, m),
+        ).start()
+    for j in range(1, m):
+        s = lax.rem(z + j, m)
+        remote(
+            parts_mp.at[s], parts_mp.at[s], sem["mesh_s"].at[j], sem["mesh_r"].at[s], "mp", z
+        ).wait_recv()
+        folded = folded + parts_mp[s]
+    squares_sum = jnp.sum(folded)
+    clip_scale = jnp.minimum(
+        1.0, 2.0 * D / jnp.sqrt(jnp.full((8, 128), squares_sum + norm_epsilon, f32))
+    )
+    total_scale = clip_scale[0:1, 0:1]
+
+    locals_in[7].wait()
+    locals_in[8].wait()
+    bias_one = 1.0 - beta_one**STEP
+    bias_two = 1.0 - beta_two**STEP
+
+    def moments(i, src):
+        b = chip(i)
+
+        def strip(at):
+            r = at(0)
+            clipped = total_scale * src[i, r].astype(f32)
+            mean = beta_one * new_first[b, r] + (1.0 - beta_one) * clipped
+            var = beta_two * new_second[b, r] + (1.0 - beta_two) * clipped * clipped
+            new_first[b, r] = mean
+            new_second[b, r] = var
+            dir_send[i, r] = (
+                mean / bias_one / (jnp.sqrt(var / bias_two) + epsilon)
+            ).astype(bf16)
+
+        strips(strip, 16)
+
+    moments(3, rot_send)
+
+    @pl.loop(0, 3)
+    def _(i):
+        received(rot_recv.at[i], sem["rot_r"].at[i])
+        moments(i, rot_recv)
+        send(dir_send.at[i], dir_recv.at[i], sem["dir_s"].at[i], sem["dir_r"].at[i], device(i))
+
+    send_low(2)
+
+    def back_slab(i, src):
+        s = device(i)
+        for t in range(2):
+            at = pl.ds(t * wide, wide)
+            back[rows(s), at] = lax.dot_general(
+                src[i], right[at, :], (((1,), (1,)), ((), ())), preferred_element_type=f32
+            ).astype(bf16)
+        send(back.at[rows(s)], back.at[rows(s)], sem["back_s"].at[i], sem["back_r"].at[i], partner)
+
+    back_slab(3, dir_send)
+
+    @pl.loop(0, 3)
+    def _(i):
+        received(dir_recv.at[i], sem["dir_r"].at[i])
+        back_slab(i, dir_recv)
+
+    for i in range(3):
+        received(low_recv.at[chip(i)], sem["low_r"].at[chip(i)])
+    for i in range(4):
+        received(back.at[rows(2 * chip(swapped[i]) + 1 - k)], sem["back_r"].at[i])
+
+    def hand_on(b, s, send_sem, target):
+        send(
+            weights.at[b, rows(s)], weights.at[b, rows(s)], send_sem, sem["out_r"].at[b * n + s], target
+        )
+
+    def arrived(b, s):
+        received(weights.at[b, rows(s)], sem["out_r"].at[b * n + s])
+
+    @pl.loop(0, nb)
+    def _(q):
+        s = 2 * q + k
+        for t in range(2):
+            at = pl.ds(t * wide, wide)
+            update = jnp.dot(left[rows(s)], back[:, at], preferred_element_type=f32)
+            weights[c, rows(s), at] = (
+                low_recv[q, :, at].astype(f32) * keep - learning_rate * update
+            ).astype(bf16)
+        hand_on(c, s, sem["out_s"].at[q], 2 * one + k)
+        hand_on(c, s, sem["out_s"].at[nb + q], 2 * two + k)
+        hand_on(c, s, sem["out_s"].at[2 * nb + q], partner)
+
+    def finish(i):
+        b = chip(i)
+
+        def strip(at):
+            r = at(0)
+            low = low_send[b, r].astype(f32)
+            new_master[b, r] = weights[b, at(me * rb)].astype(f32) + keep * (new_master[b, r] - low)
+
+        strips(strip)
+
+    finish(3)
+
+    @pl.loop(0, nb)
+    def _(q):
+        s = 2 * q + k
+        arrived(one, s)
+        hand_on(one, s, sem["pass_s"].at[q], 2 * two + k)
+        hand_on(one, s, sem["pass_s"].at[nb + q], partner)
+        arrived(two, s)
+        hand_on(two, s, sem["pass_s"].at[2 * nb + q], partner)
+
+    finish(1)
+    finish(2)
+
+    @pl.loop(0, nb)
+    def _(q):
+        s = 2 * q + k
+        arrived(chip(0), s)
+        hand_on(chip(0), s, sem["pass_s"].at[3 * nb + q], partner)
+
+    finish(0)
+
+    for i in range(4):
+        sent(pair_recv.at[i], sem["pair_s"].at[i])
+        sent(turned.at[rows(i)], sem["turned_s"].at[i])
+        sent(back.at[rows(i)], sem["back_s"].at[i])
+        sent(hop_two.at[rows(i)], sem["two_s"].at[i])
+    for i in range(3):
+        sent(rot_send.at[i], sem["rot_s"].at[i])
+        sent(dir_send.at[i], sem["dir_s"].at[i])
+        sent(low_send.at[i], sem["low_s"].at[i])
+    for i in range(7):
+        sent(right.at[rows(i)], sem["right_s"].at[i])
+        sent(left.at[rows(i)], sem["left_s"].at[i])
+    for i in range(8):
+        sent(hop_two.at[rows(0)], sem["one_s"].at[i])
+    for j in range(1, n):
+        sent(part, sem["norm_s"].at[j])
+    for j in range(1, m):
+        remote(
+            total, total, sem["mesh_s"].at[j], sem["mesh_r"].at[j], "mp", z
+        ).wait_send()
+    for i in range(12):
+        sent(weights.at[0, rows(0)], sem["out_s"].at[i])
+    for i in range(16):
+        sent(weights.at[0, rows(0)], sem["pass_s"].at[i])
+
+    @pl.loop(0, nb)
+    def _(b):
+        for q in range(nb):
+            arrived(b, 2 * q + 1 - k)
+
+
+def per_device(n, m, grad_parts, master, first_moment, second_moment, left_basis, right_basis):
+    nb, rb, cols = master.shape
+    blk = rb * n
+    args = (grad_parts, master, first_moment, second_moment, left_basis, right_basis)
+    if n != 2 * nb or nb != 4 or m > 8:
+        return per_device_general(n, m, *args)
+    bf16, f32 = jnp.bfloat16, jnp.float32
+    half = blk // 2
+    scratch = [
+        pltpu.VMEM((nb, half, cols), bf16),
+        pltpu.VMEM((nb, half, cols), bf16),
+        pltpu.VMEM((blk, cols), bf16),
+        pltpu.VMEM((blk, cols), bf16),
+        pltpu.VMEM((nb, rb, blk), bf16),
+        pltpu.VMEM((2, half, cols), bf16),
+        pltpu.VMEM((half, cols), bf16),
+        pltpu.VMEM((blk, cols), bf16),
+        pltpu.VMEM((nb, rb, cols), bf16),
+        pltpu.VMEM((nb, rb, cols), bf16),
+        pltpu.VMEM((nb, rb, cols), bf16),
+        pltpu.VMEM((nb, rb, cols), bf16),
+        pltpu.VMEM((blk, cols), bf16),
+        pltpu.VMEM((nb, rb, cols), bf16),
+        pltpu.VMEM((nb, rb, cols), bf16),
+        pltpu.VMEM((8, cols), f32),
+        pltpu.VMEM((8, 128), f32),
+        pltpu.VMEM((n, 8, 128), f32),
+        pltpu.VMEM((8, 128), f32),
+        pltpu.VMEM((m, 8, 128), f32),
+    ] + [pltpu.SemaphoreType.DMA((size,)) for _, size in SEMAPHORES]
+    shapes = [
+        jax.ShapeDtypeStruct((nb, blk, cols), bf16),
+        jax.ShapeDtypeStruct(master.shape, f32),
+        jax.ShapeDtypeStruct(master.shape, f32),
+        jax.ShapeDtypeStruct(master.shape, f32),
+    ]
+    hbm = pl.BlockSpec(memory_space=pl.ANY)
+    return pl.pallas_call(
+        functools.partial(step_kernel, n, m),
+        out_shape=shapes,
+        in_specs=[hbm] * 6,
+        out_specs=[VMEM] * 4,
+        scratch_shapes=scratch,
+        compiler_params=pltpu.CompilerParams(
+            collective_id=0, has_side_effects=True, vmem_limit_bytes=44 * 1024 * 1024
+        ),
+    )(grad_parts.reshape(nb, blk, cols), *args[1:])
+
+
 def solution(mesh):
     n, m = mesh.shape["dp"], mesh.shape["mp"]
     return jax.shard_map(

time: 229 us -> 158 us (0.69)
  waiting for transfers between devices: 66.8 us -> 0 us
  Pallas kernels: 106 us -> 143 us
  between operations: 14.9 us -> 0.65 us
  other arithmetic: 13.9 us -> 0 us
  matrix products: 13 us -> 0 us
    pallas_call x5 -> x1, Pallas kernels: 106 us -> 143 us  [per_device(): pl.pallas_call(functools.partial(step_kernel, n, m), out_shape=shapes, in...]
    all_gather x1 -> x0, waiting for transfers between devices: 34.9 us -> none  [per_device(): lax.all_gather(weight_rows, 'dp', axis=0, tiled=True).reshape(nb, blk, cols)]
    reduce_scatter x1 -> x0, waiting for transfers between devices: 31.3 us -> none  [per_device(): lax.psum_scatter(grad_parts.reshape(nb * blk, cols), 'dp', scatter_dimens...]
    dot_general x2 -> x0, matrix products: 13 us -> none  [the longest x1 7.06 us: per_device(): update = jnp.dot(left_rows, back, preferred_element_type=f32)]
    convert_element_type x2 -> x0, other arithmetic: 7.61 us -> none  [the longest x1 5.73 us: per_device(): (new_first / bias_one / (jnp.sqrt(new_second / bias_two) + epsilon)).asty...]
    reduce_sum x3 -> x0, other arithmetic: 2.98 us -> none  [the longest x1 2.37 us: per_device(): part = jnp.full((8, 128), jnp.sum(gradient * gradient), f32)]
    unnamed x15 -> x8, local copies, waits for them, and re-layouts: 13.2 us -> 14.2 us
  transfers between devices with their start and end apart: 2 -> 0, of which waited for: 2 -> 0; matrix products, arithmetic and copies ran while one was open for 2% -> 0% of each run, Pallas kernels for 30% -> 0%
where the time goes in v1:
time: 158 us
  Pallas kernels  143 us (91%)
  local copies, waits for them, and re-layouts  14.2 us (9%)
    pallas_call x1, Pallas kernels, per_device(): pl.pallas_call(functools.partial(step_kernel, n, m), out_shape=shapes, in...  143 us
    unnamed x8, local copies, waits for them, and re-layouts  14.2 us

profile of v1, /device:TPU:0, one launch (start us, length us, event | category | flops | bytes accessed | tf_op | source)
XLA Modules:
  0.0 158.2 jit_solution(11496090471140016411)
XLA Ops:
  0.6 0.0 copy-start
  0.6 1.2 copy-done
  1.9 0.0 copy-start.1
  1.9 1.2 copy-done.1
  3.1 143.4 %shard_map.93 = (bf16[4,1024,1024]{2,1,0:T(8,128)(2,1)}, f32[4,128,1024]{2,1,0:T(8,128)S(1)}, f32[4,128,1024]{2,1,0:T(8,128)S(1)}, f32[4,128,1024]{2,1,0:T(8,128)S(1)}) custom-call(bf16[4,1024,1024]{2,1,0:T(8,128)(2,1)} %bitcast.1, f32[4,128,1024]{2,1,0:T(8,128)} %master.1, f32[4,128,1024]{2,1,0:T(8,128)} %first.1, f32[4,128,1024]{2,1,0:T(8,128)} %second.1, ...), custom_call_target="tpu_custom_call" | custom-call | tf_op jit(solution)/shard_map/pallas_call | solution.py:870
  146.5 7.8 %copy.14 = bf16[4,1024,1024]{2,1,0:T(8,128)(2,1)} copy(bf16[4,1024,1024]{2,1,0:T(8,128)(2,1)} %get-tuple-element.8) | data formatting | bytes 16777216
  154.2 1.3 copy.15
  155.6 1.3 copy.16
  156.9 1.3 copy.17
Async XLA Ops:
  0.6 1.2 copy-start
  1.9 1.2 copy-start.1

commit v2 on v1

--- a/solution.py
+++ b/solution.py
@@ -383,7 +383,7 @@
 
 
 SEMAPHORES = (
-    ("local", 5),
+    ("local", 7),
     ("grad", 4),
     ("pair_s", 4),
     ("pair_r", 4),
@@ -405,6 +405,7 @@
     ("back_r", 4),
     ("low_s", 4),
     ("low_r", 4),
+    ("low_part_r", 2),
     ("out_s", 12),
     ("pass_s", 16),
     ("out_r", 32),
@@ -446,7 +447,7 @@
     squares,
     part,
     parts_dp,
-    total,
+    totals,
     parts_mp,
     *sem_refs,
 ):
@@ -487,9 +488,7 @@
         def _(t):
             body(lambda base: pl.ds(pl.multiple_of(base + t * step, step), step))
 
-    enter([("dp", n), ("mp", m)])
-
-    bases = ((right_in, right, "right", 0), (left_in, left, "left", 1))
+    bases = ((dir_send, right, "right", 4), (rot_send, left, "left", 5))
     locals_in = []
 
     def fetch(src, dst, local_sem):
@@ -497,31 +496,49 @@
         copy.start()
         locals_in.append(copy)
 
-    for x_in, x, name, _ in bases:
+    stages = []
+    for t, (src, stage) in enumerate(((right_in, dir_send), (left_in, rot_send))):
+        stages.append(pltpu.make_async_copy(src, stage, sem["local"].at[5 + t]))
+        stages[t].start()
+    for i in range(nb):
+        fetch(grad.at[chip(i), pl.ds(k * half, half)], acc.at[i], sem["grad"].at[i])
+    fetch(right_in.at[c], right.at[rows(me)], sem["local"].at[0])
+    fetch(left_in.at[c], left.at[rows(me)], sem["local"].at[1])
+    fetch(master, new_master, sem["local"].at[2])
+    fetch(first, new_first, sem["local"].at[3])
+    fetch(second, new_second, sem["local"].at[4])
+
+    z = lax.axis_index("mp")
+    z_peers = (z + 1 - 2 * lax.rem(z, 2), m - 1 - z)
+    barrier = pltpu.get_barrier_semaphore()
+    for j in range(1, n):
+        pl.semaphore_signal(
+            barrier, inc=1, device_id={"dp": lax.rem(me + j, n)}, device_id_type=MESH
+        )
+    for peer in z_peers:
+        pl.semaphore_signal(barrier, inc=1, device_id={"mp": peer}, device_id_type=MESH)
+    pl.semaphore_wait(barrier, n - 1 + len(z_peers))
+
+    for t, (stage, x, name, _) in enumerate(bases):
+        stages[t].wait()
         for i in range(3):
             send(
-                x_in.at[chip(i)],
+                stage.at[chip(i)],
                 x.at[rows(me)],
                 sem[name + "_s"].at[i],
                 sem[name + "_r"].at[me],
                 device(i),
             )
     for i in range(nb):
-        b = chip(i)
         send(
-            grad.at[b, pl.ds((1 - k) * half, half)],
+            grad.at[chip(i), pl.ds((1 - k) * half, half)],
             pair_recv.at[i],
             sem["pair_s"].at[i],
             sem["pair_r"].at[i],
             partner,
         )
-        fetch(grad.at[b, pl.ds(k * half, half)], acc.at[i], sem["grad"].at[i])
-    for x_in, x, name, slot in bases:
-        send(x_in.at[c], x.at[rows(me)], sem[name + "_s"].at[3], sem[name + "_r"].at[me], partner)
-        fetch(x_in.at[c], x.at[rows(me)], sem["local"].at[slot])
-    fetch(master, new_master, sem["local"].at[2])
-    fetch(first, new_first, sem["local"].at[3])
-    fetch(second, new_second, sem["local"].at[4])
+    for stage, x, name, _ in bases:
+        send(stage.at[c], x.at[rows(me)], sem[name + "_s"].at[3], sem[name + "_r"].at[me], partner)
 
     for i in range(nb):
         j = swapped[i]
@@ -562,6 +579,18 @@
         send(
             low_send.at[chip(i)], low_recv.at[c], sem["low_s"].at[i], sem["low_r"].at[c], device(i)
         )
+
+    def send_low_part(t):
+        part_rows = pl.ds(t * rb // 2, rb // 2)
+        send(
+            low_send.at[chip(0), part_rows],
+            low_recv.at[c, part_rows],
+            sem["low_s"].at[3 * t],
+            sem["low_part_r"].at[t],
+            device(0),
+        )
+
+    send_low(1)
 
     for _, x, name, slot in bases:
         for i in range(3):
@@ -592,9 +621,8 @@
             2 * two + k,
         )
 
-    send_low(0)
     for _, x, name, slot in bases:
-        locals_in[4 + slot].wait()
+        locals_in[slot].wait()
         for i in range(4):
             s = 2 * chip(i) + 1 - k
             received(x.at[rows(s)], sem[name + "_r"].at[s])
@@ -620,6 +648,7 @@
 
         @pl.when(q == nb - 1)
         def _():
+            send_low_part(0)
             folded = squares[:, 0:128]
             for t in range(1, cols // 128):
                 folded = folded + squares[:, t * 128 : (t + 1) * 128]
@@ -650,6 +679,22 @@
     for q in range(nb):
         received(turned.at[rows((1 - k) * nb + q)], sem["turned_r"].at[q])
 
+    def mesh_copy(t):
+        return remote(
+            totals.at[t], parts_mp.at[t], sem["mesh_s"].at[t], sem["mesh_r"].at[t], "mp", z_peers[t]
+        )
+
+    def send_total(t):
+        mesh_copy(t).start()
+
+    def receive_total(t):
+        remote(
+            parts_mp.at[t], parts_mp.at[t], sem["mesh_s"].at[t], sem["mesh_r"].at[t], "mp", z
+        ).wait_recv()
+
+    for i in range(4):
+        sent(left.at[rows(i)], sem["left_s"].at[i])
+
     @pl.loop(0, nb)
     def _(i):
         for t in range(2):
@@ -664,31 +709,21 @@
                 rot_send.at[i], rot_recv.at[i], sem["rot_s"].at[i], sem["rot_r"].at[i], device(i)
             )
 
-    send_low(1)
-
-    folded = part[...]
-    for j in range(1, n):
-        s = lax.rem(me + j, n)
-        received(parts_dp.at[s], sem["norm_r"].at[s])
-        folded = folded + parts_dp[s]
-    total[...] = folded
-    z = lax.axis_index("mp")
-    for j in range(1, m):
-        remote(
-            total,
-            parts_mp.at[z],
-            sem["mesh_s"].at[j],
-            sem["mesh_r"].at[z],
-            "mp",
-            lax.rem(z + j, m),
-        ).start()
-    for j in range(1, m):
-        s = lax.rem(z + j, m)
-        remote(
-            parts_mp.at[s], parts_mp.at[s], sem["mesh_s"].at[j], sem["mesh_r"].at[s], "mp", z
-        ).wait_recv()
-        folded = folded + parts_mp[s]
-    squares_sum = jnp.sum(folded)
+        @pl.when(i == 0)
+        def _():
+            folded = part[...]
+            for j in range(1, n):
+                s = lax.rem(me + j, n)
+                received(parts_dp.at[s], sem["norm_r"].at[s])
+                folded = folded + parts_dp[s]
+            totals[0] = folded
+            send_total(0)
+
+    receive_total(0)
+    totals[1] = totals[0] + parts_mp[0]
+    send_total(1)
+    receive_total(1)
+    squares_sum = jnp.sum(totals[1] + parts_mp[1])
     clip_scale = jnp.minimum(
         1.0, 2.0 * D / jnp.sqrt(jnp.full((8, 128), squares_sum + norm_epsilon, f32))
     )
@@ -715,6 +750,8 @@
 
         strips(strip, 16)
 
+    for i in range(4):
+        sent(right.at[rows(i)], sem["right_s"].at[i])
     moments(3, rot_send)
 
     @pl.loop(0, 3)
@@ -722,8 +759,6 @@
         received(rot_recv.at[i], sem["rot_r"].at[i])
         moments(i, rot_recv)
         send(dir_send.at[i], dir_recv.at[i], sem["dir_s"].at[i], sem["dir_r"].at[i], device(i))
-
-    send_low(2)
 
     def back_slab(i, src):
         s = device(i)
@@ -739,10 +774,14 @@
     @pl.loop(0, 3)
     def _(i):
         received(dir_recv.at[i], sem["dir_r"].at[i])
+
+        @pl.when(i == 0)
+        def _():
+            send_low(2)
+            send_low_part(1)
+
         back_slab(i, dir_recv)
 
-    for i in range(3):
-        received(low_recv.at[chip(i)], sem["low_r"].at[chip(i)])
     for i in range(4):
         received(back.at[rows(2 * chip(swapped[i]) + 1 - k)], sem["back_r"].at[i])
 
@@ -754,14 +793,28 @@
     def arrived(b, s):
         received(weights.at[b, rows(s)], sem["out_r"].at[b * n + s])
 
+    def relative(first_flip, second_flip):
+        return c + first_flip * (one - c) + second_flip * (two - c)
+
     @pl.loop(0, nb)
     def _(q):
-        s = 2 * q + k
+        b = relative(q % 2, q // 2)
+        s = 2 * b + k
+
+        @pl.when((q == 1) + (q == 2) > 0)
+        def _():
+            received(low_recv.at[b], sem["low_r"].at[b])
+
+        @pl.when(q == 3)
+        def _():
+            for t in range(2):
+                received(low_recv.at[b, pl.ds(0, rb // 2)], sem["low_part_r"].at[t])
+
         for t in range(2):
             at = pl.ds(t * wide, wide)
             update = jnp.dot(left[rows(s)], back[:, at], preferred_element_type=f32)
             weights[c, rows(s), at] = (
-                low_recv[q, :, at].astype(f32) * keep - learning_rate * update
+                low_recv[b, :, at].astype(f32) * keep - learning_rate * update
             ).astype(bf16)
         hand_on(c, s, sem["out_s"].at[q], 2 * one + k)
         hand_on(c, s, sem["out_s"].at[nb + q], 2 * two + k)
@@ -779,21 +832,20 @@
 
     finish(3)
 
-    @pl.loop(0, nb)
-    def _(q):
-        s = 2 * q + k
+    for q in range(nb):
+        s = 2 * relative(1 - q % 2, q // 2) + k
         arrived(one, s)
         hand_on(one, s, sem["pass_s"].at[q], 2 * two + k)
         hand_on(one, s, sem["pass_s"].at[nb + q], partner)
+        s = 2 * relative(q % 2, 1 - q // 2) + k
         arrived(two, s)
         hand_on(two, s, sem["pass_s"].at[2 * nb + q], partner)
 
     finish(1)
     finish(2)
 
-    @pl.loop(0, nb)
-    def _(q):
-        s = 2 * q + k
+    for q in range(nb):
+        s = 2 * relative(1 - q % 2, 1 - q // 2) + k
         arrived(chip(0), s)
         hand_on(chip(0), s, sem["pass_s"].at[3 * nb + q], partner)
 
@@ -807,18 +859,18 @@
     for i in range(3):
         sent(rot_send.at[i], sem["rot_s"].at[i])
         sent(dir_send.at[i], sem["dir_s"].at[i])
+        sent(right.at[rows(i)], sem["right_s"].at[4 + i])
+        sent(left.at[rows(i)], sem["left_s"].at[4 + i])
+    for i in (1, 2):
         sent(low_send.at[i], sem["low_s"].at[i])
-    for i in range(7):
-        sent(right.at[rows(i)], sem["right_s"].at[i])
-        sent(left.at[rows(i)], sem["left_s"].at[i])
+    for t in range(2):
+        sent(low_send.at[0, pl.ds(0, rb // 2)], sem["low_s"].at[3 * t])
     for i in range(8):
         sent(hop_two.at[rows(0)], sem["one_s"].at[i])
     for j in range(1, n):
         sent(part, sem["norm_s"].at[j])
-    for j in range(1, m):
-        remote(
-            total, total, sem["mesh_s"].at[j], sem["mesh_r"].at[j], "mp", z
-        ).wait_send()
+    for t in range(2):
+        mesh_copy(t).wait_send()
     for i in range(12):
         sent(weights.at[0, rows(0)], sem["out_s"].at[i])
     for i in range(16):
@@ -830,11 +882,24 @@
             arrived(b, 2 * q + 1 - k)
 
 
+def store_kernel(weights, master, first, second, weights_out, master_out, first_out, second_out, sem):
+    nb = weights.shape[0]
+    pairs = [(weights.at[b], weights_out.at[b]) for b in range(nb)]
+    pairs += [(master, master_out), (first, first_out), (second, second_out)]
+    copies = [
+        pltpu.make_async_copy(src, dst, sem.at[i]) for i, (src, dst) in enumerate(pairs)
+    ]
+    for copy in copies:
+        copy.start()
+    for copy in copies:
+        copy.wait()
+
+
 def per_device(n, m, grad_parts, master, first_moment, second_moment, left_basis, right_basis):
     nb, rb, cols = master.shape
     blk = rb * n
     args = (grad_parts, master, first_moment, second_moment, left_basis, right_basis)
-    if n != 2 * nb or nb != 4 or m > 8:
+    if n != 2 * nb or nb != 4 or m != 4:
         return per_device_general(n, m, *args)
     bf16, f32 = jnp.bfloat16, jnp.float32
     half = blk // 2
@@ -857,8 +922,8 @@
         pltpu.VMEM((8, cols), f32),
         pltpu.VMEM((8, 128), f32),
         pltpu.VMEM((n, 8, 128), f32),
-        pltpu.VMEM((8, 128), f32),
-        pltpu.VMEM((m, 8, 128), f32),
+        pltpu.VMEM((2, 8, 128), f32),
+        pltpu.VMEM((2, 8, 128), f32),
     ] + [pltpu.SemaphoreType.DMA((size,)) for _, size in SEMAPHORES]
     shapes = [
         jax.ShapeDtypeStruct((nb, blk, cols), bf16),
@@ -866,10 +931,10 @@
         jax.ShapeDtypeStruct(master.shape, f32),
         jax.ShapeDtypeStruct(master.shape, f32),
     ]
-    hbm = pl.BlockSpec(memory_space=pl.ANY)
-    return pl.pallas_call(
+    hbm = pl.BlockSpec(memory_space=pltpu.HBM)
+    results = pl.pallas_call(
         functools.partial(step_kernel, n, m),
-        out_shape=shapes,
+        out_shape=[pltpu.VMEM(shape.shape, shape.dtype) for shape in shapes],
         in_specs=[hbm] * 6,
         out_specs=[VMEM] * 4,
         scratch_shapes=scratch,
@@ -877,6 +942,14 @@
             collective_id=0, has_side_effects=True, vmem_limit_bytes=44 * 1024 * 1024
         ),
     )(grad_parts.reshape(nb, blk, cols), *args[1:])
+    return pl.pallas_call(
+        store_kernel,
+        out_shape=shapes,
+        in_specs=[VMEM] * 4,
+        out_specs=[hbm] * 4,
+        scratch_shapes=[pltpu.SemaphoreType.DMA((nb + 3,))],
+        compiler_params=pltpu.CompilerParams(vmem_limit_bytes=1024 * 1024),
+    )(*results)
 
 
 def solution(mesh):

time: 158 us -> 141 us (0.89)
  local copies, waits for them, and re-layouts: 14.2 us -> 0 us
  Pallas kernels: 143 us -> 141 us
    unnamed x8 -> x0, local copies, waits for them, and re-layouts: 14.2 us -> none
    pallas_call x1 -> x2, Pallas kernels: 143 us -> 141 us  [the longest x1 135 us: per_device(): pl.pallas_call(functools.partial(step_kernel, n, m), out_shape=[pltpu.VME...]
where the time goes in v2:
time: 141 us
  Pallas kernels  141 us (100%)
    pallas_call x1, Pallas kernels, per_device(): pl.pallas_call(functools.partial(step_kernel, n, m), out_shape=[pltpu.VME...  135 us
    pallas_call x1, Pallas kernels, per_device(): pl.pallas_call(store_kernel, out_shape=shapes, in_specs=[VMEM] * 4, out_s...  5.29 us

profile of v2, /device:TPU:0, one launch (start us, length us, event | category | flops | bytes accessed | tf_op | source)
XLA Modules:
  0.0 141.3 jit_solution(3763971110379766480)
XLA Ops:
  0.6 135.4 %shard_map.93 = (bf16[4,1024,1024]{2,1,0:T(8,128)(2,1)S(1)}, f32[4,128,1024]{2,1,0:T(8,128)S(1)}, f32[4,128,1024]{2,1,0:T(8,128)S(1)}, f32[4,128,1024]{2,1,0:T(8,128)S(1)}) custom-call(bf16[4,1024,1024]{2,1,0:T(8,128)(2,1)} %bitcast.1, f32[4,128,1024]{2,1,0:T(8,128)} %master.1, f32[4,128,1024]{2,1,0:T(8,128)} %first.1, f32[4,128,1024]{2,1,0:T(8,128)} %second.1, ...), custom_call_target="tpu_custom_call" | custom-call | tf_op jit(solution)/shard_map/pallas_call | solution.py:935
  136.0 5.3 %shard_map.94 = (bf16[4,1024,1024]{2,1,0:T(8,128)(2,1)}, f32[4,128,1024]{2,1,0:T(8,128)}, f32[4,128,1024]{2,1,0:T(8,128)}, f32[4,128,1024]{2,1,0:T(8,128)}) custom-call(bf16[4,1024,1024]{2,1,0:T(8,128)(2,1)S(1)} %get-tuple-element.8.weights, f32[4,128,1024]{2,1,0:T(8,128)S(1)} %get-tuple-element.9.master, f32[4,128,1024]{2,1,0:T(8,128)S(1)} %get-tuple-element.10.first, ...), custom_call_target="tpu_custom_call" | custom-call | tf_op jit(solution)/shard_map/pallas_call | solution.py:945

commit v3 on v2

--- a/solution.py
+++ b/solution.py
@@ -385,34 +385,37 @@
 SEMAPHORES = (
     ("local", 7),
     ("grad", 4),
-    ("pair_s", 4),
+    ("pair_s", 1),
     ("pair_r", 4),
-    ("right_s", 8),
-    ("right_r", 8),
-    ("left_s", 8),
-    ("left_r", 8),
-    ("one_s", 8),
+    ("right_s", 1),
+    ("right_r", 3),
+    ("right_pass_r", 1),
+    ("left_s", 1),
+    ("left_r", 3),
+    ("left_pass_r", 1),
+    ("pass_bases_s", 1),
+    ("one_s", 1),
     ("one_r", 8),
-    ("two_s", 4),
+    ("two_s", 1),
     ("two_r", 4),
-    ("turned_s", 4),
-    ("turned_r", 4),
-    ("rot_s", 4),
-    ("rot_r", 4),
-    ("dir_s", 4),
-    ("dir_r", 4),
-    ("back_s", 4),
-    ("back_r", 4),
-    ("low_s", 4),
-    ("low_r", 4),
-    ("low_part_r", 2),
-    ("out_s", 12),
-    ("pass_s", 16),
-    ("out_r", 32),
-    ("norm_s", 8),
-    ("norm_r", 8),
-    ("mesh_s", 8),
-    ("mesh_r", 8),
+    ("turned_s", 1),
+    ("turned_r", 1),
+    ("rot_s", 1),
+    ("rot_r", 3),
+    ("dir_s", 1),
+    ("dir_r", 3),
+    ("back_s", 1),
+    ("back_r", 1),
+    ("low_s", 1),
+    ("low_r", 3),
+    ("out_s", 1),
+    ("pass_s", 1),
+    ("out_r", 12),
+    ("out_pass_r", 1),
+    ("norm_s", 1),
+    ("norm_r", 1),
+    ("mesh_s", 1),
+    ("mesh_r", 3),
 )
 
 
@@ -498,7 +501,7 @@
 
     stages = []
     for t, (src, stage) in enumerate(((right_in, dir_send), (left_in, rot_send))):
-        stages.append(pltpu.make_async_copy(src, stage, sem["local"].at[5 + t]))
+        stages.append(pltpu.make_async_copy(src, stage, sem["local"].at[4 + t]))
         stages[t].start()
     for i in range(nb):
         fetch(grad.at[chip(i), pl.ds(k * half, half)], acc.at[i], sem["grad"].at[i])
@@ -506,18 +509,24 @@
     fetch(left_in.at[c], left.at[rows(me)], sem["local"].at[1])
     fetch(master, new_master, sem["local"].at[2])
     fetch(first, new_first, sem["local"].at[3])
-    fetch(second, new_second, sem["local"].at[4])
+    fetch(second, new_second, sem["local"].at[6])
 
     z = lax.axis_index("mp")
-    z_peers = (z + 1 - 2 * lax.rem(z, 2), m - 1 - z)
     barrier = pltpu.get_barrier_semaphore()
     for j in range(1, n):
         pl.semaphore_signal(
             barrier, inc=1, device_id={"dp": lax.rem(me + j, n)}, device_id_type=MESH
         )
-    for peer in z_peers:
-        pl.semaphore_signal(barrier, inc=1, device_id={"mp": peer}, device_id_type=MESH)
-    pl.semaphore_wait(barrier, n - 1 + len(z_peers))
+
+    @pl.when(z == 0)
+    def _():
+        for j in range(1, m):
+            pl.semaphore_signal(barrier, inc=1, device_id={"mp": j}, device_id_type=MESH)
+        pl.semaphore_wait(barrier, n - 1)
+
+    @pl.when(z > 0)
+    def _():
+        pl.semaphore_wait(barrier, n)
 
     for t, (stage, x, name, _) in enumerate(bases):
         stages[t].wait()
@@ -525,20 +534,22 @@
             send(
                 stage.at[chip(i)],
                 x.at[rows(me)],
-                sem[name + "_s"].at[i],
-                sem[name + "_r"].at[me],
+                sem[name + "_s"].at[0],
+                sem[name + "_r"].at[i],
                 device(i),
             )
     for i in range(nb):
         send(
             grad.at[chip(i), pl.ds((1 - k) * half, half)],
             pair_recv.at[i],
-            sem["pair_s"].at[i],
+            sem["pair_s"].at[0],
             sem["pair_r"].at[i],
             partner,
         )
     for stage, x, name, _ in bases:
-        send(stage.at[c], x.at[rows(me)], sem[name + "_s"].at[3], sem[name + "_r"].at[me], partner)
+        send(
+            stage.at[c], x.at[rows(me)], sem[name + "_s"].at[0], sem[name + "_pass_r"].at[0], partner
+        )
 
     for i in range(nb):
         j = swapped[i]
@@ -556,7 +567,7 @@
                 send(
                     acc.at[i, rows(q)],
                     hop_one.at[i, rows(q)],
-                    sem["one_s"].at[i * nb + q],
+                    sem["one_s"].at[0],
                     sem["one_r"].at[i * nb + q],
                     2 * one + k,
                 )
@@ -577,7 +588,7 @@
 
     def send_low(i):
         send(
-            low_send.at[chip(i)], low_recv.at[c], sem["low_s"].at[i], sem["low_r"].at[c], device(i)
+            low_send.at[chip(i)], low_recv.at[c], sem["low_s"].at[0], sem["low_r"].at[i], device(i)
         )
 
     def send_low_part(t):
@@ -585,8 +596,8 @@
         send(
             low_send.at[chip(0), part_rows],
             low_recv.at[c, part_rows],
-            sem["low_s"].at[3 * t],
-            sem["low_part_r"].at[t],
+            sem["low_s"].at[0],
+            sem["low_r"].at[0],
             device(0),
         )
 
@@ -595,12 +606,12 @@
     for _, x, name, slot in bases:
         for i in range(3):
             s = device(i)
-            received(x.at[rows(s)], sem[name + "_r"].at[s])
+            received(x.at[rows(s)], sem[name + "_r"].at[i])
             send(
                 x.at[rows(s)],
                 x.at[rows(s)],
-                sem[name + "_s"].at[4 + i],
-                sem[name + "_r"].at[s],
+                sem["pass_bases_s"].at[0],
+                sem[name + "_pass_r"].at[0],
                 partner,
             )
 
@@ -616,16 +627,14 @@
         send(
             acc.at[2, rows(q)],
             hop_two.at[rows(q)],
-            sem["two_s"].at[q],
+            sem["two_s"].at[0],
             sem["two_r"].at[q],
             2 * two + k,
         )
 
     for _, x, name, slot in bases:
         locals_in[slot].wait()
-        for i in range(4):
-            s = 2 * chip(i) + 1 - k
-            received(x.at[rows(s)], sem[name + "_r"].at[s])
+        received(x.at[pl.ds(0, half)], sem[name + "_pass_r"].at[0])
 
     @pl.loop(0, nb)
     def _(i):
@@ -657,8 +666,8 @@
                 send(
                     part,
                     parts_dp.at[me],
-                    sem["norm_s"].at[j],
-                    sem["norm_r"].at[me],
+                    sem["norm_s"].at[0],
+                    sem["norm_r"].at[0],
                     lax.rem(me + j, n),
                 )
 
@@ -671,29 +680,19 @@
         send(
             turned.at[rows(s)],
             turned.at[rows(s)],
-            sem["turned_s"].at[q],
-            sem["turned_r"].at[q],
+            sem["turned_s"].at[0],
+            sem["turned_r"].at[0],
             partner,
         )
 
-    for q in range(nb):
-        received(turned.at[rows((1 - k) * nb + q)], sem["turned_r"].at[q])
-
-    def mesh_copy(t):
+    received(turned.at[pl.ds((1 - k) * half, half)], sem["turned_r"].at[0])
+
+    def mesh_copy(t, slot, target):
         return remote(
-            totals.at[t], parts_mp.at[t], sem["mesh_s"].at[t], sem["mesh_r"].at[t], "mp", z_peers[t]
-        )
-
-    def send_total(t):
-        mesh_copy(t).start()
-
-    def receive_total(t):
-        remote(
-            parts_mp.at[t], parts_mp.at[t], sem["mesh_s"].at[t], sem["mesh_r"].at[t], "mp", z
-        ).wait_recv()
-
-    for i in range(4):
-        sent(left.at[rows(i)], sem["left_s"].at[i])
+            totals.at[t], parts_mp.at[slot], sem["mesh_s"].at[0], sem["mesh_r"].at[slot], "mp", target
+        )
+
+    sent(rot_send, sem["left_s"].at[0])
 
     @pl.loop(0, nb)
     def _(i):
@@ -706,24 +705,37 @@
         @pl.when(i < 3)
         def _():
             send(
-                rot_send.at[i], rot_recv.at[i], sem["rot_s"].at[i], sem["rot_r"].at[i], device(i)
+                rot_send.at[i], rot_recv.at[i], sem["rot_s"].at[0], sem["rot_r"].at[i], device(i)
             )
 
         @pl.when(i == 0)
         def _():
             folded = part[...]
+            received(parts_dp.at[pl.ds(0, n - 1)], sem["norm_r"].at[0])
             for j in range(1, n):
-                s = lax.rem(me + j, n)
-                received(parts_dp.at[s], sem["norm_r"].at[s])
-                folded = folded + parts_dp[s]
+                folded = folded + parts_dp[lax.rem(me + j, n)]
             totals[0] = folded
-            send_total(0)
-
-    receive_total(0)
-    totals[1] = totals[0] + parts_mp[0]
-    send_total(1)
-    receive_total(1)
-    squares_sum = jnp.sum(totals[1] + parts_mp[1])
+
+            @pl.when(z > 0)
+            def _():
+                mesh_copy(0, z - 1, 0).start()
+
+    @pl.when(z == 0)
+    def _():
+        folded = totals[0]
+        for j in range(1, m):
+            mesh_copy(0, j - 1, 0).wait_recv()
+            folded = folded + parts_mp[j - 1]
+        totals[1] = folded
+        for j in range(1, m):
+            mesh_copy(1, 0, j).start()
+
+    @pl.when(z > 0)
+    def _():
+        mesh_copy(1, 0, 0).wait_recv()
+        totals[1] = parts_mp[0]
+
+    squares_sum = jnp.sum(totals[1])
     clip_scale = jnp.minimum(
         1.0, 2.0 * D / jnp.sqrt(jnp.full((8, 128), squares_sum + norm_epsilon, f32))
     )
@@ -750,15 +762,14 @@
 
         strips(strip, 16)
 
-    for i in range(4):
-        sent(right.at[rows(i)], sem["right_s"].at[i])
+    sent(dir_send, sem["right_s"].at[0])
     moments(3, rot_send)
 
     @pl.loop(0, 3)
     def _(i):
         received(rot_recv.at[i], sem["rot_r"].at[i])
         moments(i, rot_recv)
-        send(dir_send.at[i], dir_recv.at[i], sem["dir_s"].at[i], sem["dir_r"].at[i], device(i))
+        send(dir_send.at[i], dir_recv.at[i], sem["dir_s"].at[0], sem["dir_r"].at[i], device(i))
 
     def back_slab(i, src):
         s = device(i)
@@ -767,7 +778,7 @@
             back[rows(s), at] = lax.dot_general(
                 src[i], right[at, :], (((1,), (1,)), ((), ())), preferred_element_type=f32
             ).astype(bf16)
-        send(back.at[rows(s)], back.at[rows(s)], sem["back_s"].at[i], sem["back_r"].at[i], partner)
+        send(back.at[rows(s)], back.at[rows(s)], sem["back_s"].at[0], sem["back_r"].at[0], partner)
 
     back_slab(3, dir_send)
 
@@ -782,16 +793,15 @@
 
         back_slab(i, dir_recv)
 
-    for i in range(4):
-        received(back.at[rows(2 * chip(swapped[i]) + 1 - k)], sem["back_r"].at[i])
-
-    def hand_on(b, s, send_sem, target):
-        send(
-            weights.at[b, rows(s)], weights.at[b, rows(s)], send_sem, sem["out_r"].at[b * n + s], target
-        )
-
-    def arrived(b, s):
-        received(weights.at[b, rows(s)], sem["out_r"].at[b * n + s])
+    received(back.at[pl.ds(0, half)], sem["back_r"].at[0])
+
+    def hand_on(b, s, name, recv_sem, target):
+        send(weights.at[b, rows(s)], weights.at[b, rows(s)], sem[name].at[0], recv_sem, target)
+
+    def slot(t, q):
+        return sem["out_r"].at[t * nb + q]
+
+    to_partner = sem["out_pass_r"].at[0]
 
     def relative(first_flip, second_flip):
         return c + first_flip * (one - c) + second_flip * (two - c)
@@ -803,12 +813,11 @@
 
         @pl.when((q == 1) + (q == 2) > 0)
         def _():
-            received(low_recv.at[b], sem["low_r"].at[b])
+            received(low_recv.at[b], sem["low_r"].at[q])
 
         @pl.when(q == 3)
         def _():
-            for t in range(2):
-                received(low_recv.at[b, pl.ds(0, rb // 2)], sem["low_part_r"].at[t])
+            received(low_recv.at[b], sem["low_r"].at[0])
 
         for t in range(2):
             at = pl.ds(t * wide, wide)
@@ -816,9 +825,9 @@
             weights[c, rows(s), at] = (
                 low_recv[b, :, at].astype(f32) * keep - learning_rate * update
             ).astype(bf16)
-        hand_on(c, s, sem["out_s"].at[q], 2 * one + k)
-        hand_on(c, s, sem["out_s"].at[nb + q], 2 * two + k)
-        hand_on(c, s, sem["out_s"].at[2 * nb + q], partner)
+        hand_on(c, s, "out_s", slot(0, q), 2 * one + k)
+        hand_on(c, s, "out_s", slot(1, q), 2 * two + k)
+        hand_on(c, s, "out_s", to_partner, partner)
 
     def finish(i):
         b = chip(i)
@@ -834,52 +843,48 @@
 
     for q in range(nb):
         s = 2 * relative(1 - q % 2, q // 2) + k
-        arrived(one, s)
-        hand_on(one, s, sem["pass_s"].at[q], 2 * two + k)
-        hand_on(one, s, sem["pass_s"].at[nb + q], partner)
+        received(weights.at[one, rows(s)], slot(0, q))
+        hand_on(one, s, "pass_s", slot(2, q), 2 * two + k)
+        hand_on(one, s, "pass_s", to_partner, partner)
         s = 2 * relative(q % 2, 1 - q // 2) + k
-        arrived(two, s)
-        hand_on(two, s, sem["pass_s"].at[2 * nb + q], partner)
+        received(weights.at[two, rows(s)], slot(1, q))
+        hand_on(two, s, "pass_s", to_partner, partner)
 
     finish(1)
     finish(2)
 
     for q in range(nb):
         s = 2 * relative(1 - q % 2, 1 - q // 2) + k
-        arrived(chip(0), s)
-        hand_on(chip(0), s, sem["pass_s"].at[3 * nb + q], partner)
+        received(weights.at[chip(0), rows(s)], slot(2, q))
+        hand_on(chip(0), s, "pass_s", to_partner, partner)
 
     finish(0)
 
-    for i in range(4):
-        sent(pair_recv.at[i], sem["pair_s"].at[i])
-        sent(turned.at[rows(i)], sem["turned_s"].at[i])
-        sent(back.at[rows(i)], sem["back_s"].at[i])
-        sent(hop_two.at[rows(i)], sem["two_s"].at[i])
-    for i in range(3):
-        sent(rot_send.at[i], sem["rot_s"].at[i])
-        sent(dir_send.at[i], sem["dir_s"].at[i])
-        sent(right.at[rows(i)], sem["right_s"].at[4 + i])
-        sent(left.at[rows(i)], sem["left_s"].at[4 + i])
-    for i in (1, 2):
-        sent(low_send.at[i], sem["low_s"].at[i])
-    for t in range(2):
-        sent(low_send.at[0, pl.ds(0, rb // 2)], sem["low_s"].at[3 * t])
-    for i in range(8):
-        sent(hop_two.at[rows(0)], sem["one_s"].at[i])
-    for j in range(1, n):
-        sent(part, sem["norm_s"].at[j])
-    for t in range(2):
-        mesh_copy(t).wait_send()
-    for i in range(12):
-        sent(weights.at[0, rows(0)], sem["out_s"].at[i])
-    for i in range(16):
-        sent(weights.at[0, rows(0)], sem["pass_s"].at[i])
-
-    @pl.loop(0, nb)
-    def _(b):
-        for q in range(nb):
-            arrived(b, 2 * q + 1 - k)
+    for ref, name in (
+        (pair_recv, "pair_s"),
+        (hop_one, "one_s"),
+        (hop_two, "two_s"),
+        (turned.at[pl.ds(0, half)], "turned_s"),
+        (back.at[pl.ds(0, half)], "back_s"),
+        (rot_send.at[pl.ds(0, 3)], "rot_s"),
+        (dir_send.at[pl.ds(0, 3)], "dir_s"),
+        (low_send.at[pl.ds(0, 3)], "low_s"),
+        (left.at[pl.ds(0, 6 * rb)], "pass_bases_s"),
+        (parts_dp.at[pl.ds(0, n - 1)], "norm_s"),
+        (acc.at[pl.ds(0, 3)], "out_s"),
+        (weights.at[pl.ds(0, 2)], "pass_s"),
+    ):
+        sent(ref, sem[name].at[0])
+
+    @pl.when(z == 0)
+    def _():
+        sent(parts_mp, sem["mesh_s"].at[0])
+
+    @pl.when(z > 0)
+    def _():
+        sent(totals.at[0], sem["mesh_s"].at[0])
+
+    received(weights.at[pl.ds(0, 2)], to_partner)
 
 
 def store_kernel(weights, master, first, second, weights_out, master_out, first_out, second_out, sem):
@@ -923,7 +928,7 @@
         pltpu.VMEM((8, 128), f32),
         pltpu.VMEM((n, 8, 128), f32),
         pltpu.VMEM((2, 8, 128), f32),
-        pltpu.VMEM((2, 8, 128), f32),
+        pltpu.VMEM((m - 1, 8, 128), f32),
     ] + [pltpu.SemaphoreType.DMA((size,)) for _, size in SEMAPHORES]
     shapes = [
         jax.ShapeDtypeStruct((nb, blk, cols), bf16),

time: 141 us -> 138 us (0.979)
  Pallas kernels: 141 us -> 137 us
    pallas_call x1, Pallas kernels: 135 us -> 132 us  [per_device(): pl.pallas_call(functools.partial(step_kernel, n, m), out_shape=[pltpu.VME...]
where the time goes in v3:
time: 138 us
  Pallas kernels  137 us (99%)
    pallas_call x1, Pallas kernels, per_device(): pl.pallas_call(functools.partial(step_kernel, n, m), out_shape=[pltpu.VME...  132 us
    pallas_call x1, Pallas kernels, per_device(): pl.pallas_call(store_kernel, out_shape=shapes, in_specs=[VMEM] * 4, out_s...  5.29 us

profile of v3, /device:TPU:0, one launch (start us, length us, event | category | flops | bytes accessed | tf_op | source)
XLA Modules:
  0.0 137.8 jit_solution(531300535948165210)
XLA Ops:
  0.6 131.9 %shard_map.93 = (bf16[4,1024,1024]{2,1,0:T(8,128)(2,1)S(1)}, f32[4,128,1024]{2,1,0:T(8,128)S(1)}, f32[4,128,1024]{2,1,0:T(8,128)S(1)}, f32[4,128,1024]{2,1,0:T(8,128)S(1)}) custom-call(bf16[4,1024,1024]{2,1,0:T(8,128)(2,1)} %bitcast.1, f32[4,128,1024]{2,1,0:T(8,128)} %master.1, f32[4,128,1024]{2,1,0:T(8,128)} %first.1, f32[4,128,1024]{2,1,0:T(8,128)} %second.1, ...), custom_call_target="tpu_custom_call" | custom-call | tf_op jit(solution)/shard_map/pallas_call | solution.py:940
  132.5 5.3 %shard_map.94 = (bf16[4,1024,1024]{2,1,0:T(8,128)(2,1)}, f32[4,128,1024]{2,1,0:T(8,128)}, f32[4,128,1024]{2,1,0:T(8,128)}, f32[4,128,1024]{2,1,0:T(8,128)}) custom-call(bf16[4,1024,1024]{2,1,0:T(8,128)(2,1)S(1)} %get-tuple-element.8.weights, f32[4,128,1024]{2,1,0:T(8,128)S(1)} %get-tuple-element.9.master, f32[4,128,1024]{2,1,0:T(8,128)S(1)} %get-tuple-element.10.first, ...), custom_call_target="tpu_custom_call" | custom-call | tf_op jit(solution)/shard_map/pallas_call | solution.py:950

commit v4 on v3

--- a/solution.py
+++ b/solution.py
@@ -384,9 +384,9 @@
 
 SEMAPHORES = (
     ("local", 7),
-    ("grad", 4),
+    ("grad", 1),
     ("pair_s", 1),
-    ("pair_r", 4),
+    ("pair_r", 1),
     ("right_s", 1),
     ("right_r", 3),
     ("right_pass_r", 1),
@@ -395,7 +395,7 @@
     ("left_pass_r", 1),
     ("pass_bases_s", 1),
     ("one_s", 1),
-    ("one_r", 8),
+    ("one_r", 4),
     ("two_s", 1),
     ("two_r", 4),
     ("turned_s", 1),
@@ -410,7 +410,7 @@
     ("low_r", 3),
     ("out_s", 1),
     ("pass_s", 1),
-    ("out_r", 12),
+    ("out_r", 15),
     ("out_pass_r", 1),
     ("norm_s", 1),
     ("norm_r", 1),
@@ -504,7 +504,7 @@
         stages.append(pltpu.make_async_copy(src, stage, sem["local"].at[4 + t]))
         stages[t].start()
     for i in range(nb):
-        fetch(grad.at[chip(i), pl.ds(k * half, half)], acc.at[i], sem["grad"].at[i])
+        fetch(grad.at[chip(i), pl.ds(k * half, half)], acc.at[i], sem["grad"].at[0])
     fetch(right_in.at[c], right.at[rows(me)], sem["local"].at[0])
     fetch(left_in.at[c], left.at[rows(me)], sem["local"].at[1])
     fetch(master, new_master, sem["local"].at[2])
@@ -513,37 +513,39 @@
 
     z = lax.axis_index("mp")
     barrier = pltpu.get_barrier_semaphore()
-    for j in range(1, n):
-        pl.semaphore_signal(
-            barrier, inc=1, device_id={"dp": lax.rem(me + j, n)}, device_id_type=MESH
-        )
+    for target in (device(1), device(2), partner):
+        pl.semaphore_signal(barrier, inc=1, device_id={"dp": target}, device_id_type=MESH)
 
     @pl.when(z == 0)
     def _():
         for j in range(1, m):
             pl.semaphore_signal(barrier, inc=1, device_id={"mp": j}, device_id_type=MESH)
-        pl.semaphore_wait(barrier, n - 1)
+        pl.semaphore_wait(barrier, 3)
 
     @pl.when(z > 0)
     def _():
-        pl.semaphore_wait(barrier, n)
-
-    for t, (stage, x, name, _) in enumerate(bases):
+        pl.semaphore_wait(barrier, 4)
+
+    def send_base(t, i):
+        stage, x, name, _ = bases[t]
+        send(
+            stage.at[chip(i)],
+            x.at[rows(me)],
+            sem[name + "_s"].at[0],
+            sem[name + "_r"].at[i],
+            device(i),
+        )
+
+    for t in range(2):
         stages[t].wait()
-        for i in range(3):
-            send(
-                stage.at[chip(i)],
-                x.at[rows(me)],
-                sem[name + "_s"].at[0],
-                sem[name + "_r"].at[i],
-                device(i),
-            )
+        send_base(t, 1)
+        send_base(t, 2)
     for i in range(nb):
         send(
             grad.at[chip(i), pl.ds((1 - k) * half, half)],
             pair_recv.at[i],
             sem["pair_s"].at[0],
-            sem["pair_r"].at[i],
+            sem["pair_r"].at[0],
             partner,
         )
     for stage, x, name, _ in bases:
@@ -551,10 +553,27 @@
             stage.at[c], x.at[rows(me)], sem[name + "_s"].at[0], sem[name + "_pass_r"].at[0], partner
         )
 
+    def pass_base(t, i):
+        _, x, name, _ = bases[t]
+        s = device(i)
+        received(x.at[rows(s)], sem[name + "_r"].at[i])
+        send(
+            x.at[rows(s)],
+            x.at[rows(s)],
+            sem["pass_bases_s"].at[0],
+            sem[name + "_pass_r"].at[0],
+            partner,
+        )
+
+    pass_base(0, 1)
+    pass_base(0, 2)
+    send_base(0, 0)
+    send_base(1, 0)
+
+    pltpu.make_async_copy(pair_recv, acc, sem["grad"].at[0]).wait()
+    received(pair_recv, sem["pair_r"].at[0])
     for i in range(nb):
         j = swapped[i]
-        locals_in[i].wait()
-        received(pair_recv.at[j], sem["pair_r"].at[j])
 
         @pl.loop(0, nb)
         def _(q):
@@ -568,7 +587,7 @@
                     acc.at[i, rows(q)],
                     hop_one.at[i, rows(q)],
                     sem["one_s"].at[0],
-                    sem["one_r"].at[i * nb + q],
+                    sem["one_r" if i == 0 else "two_r"].at[q],
                     2 * one + k,
                 )
 
@@ -603,17 +622,8 @@
 
     send_low(1)
 
-    for _, x, name, slot in bases:
-        for i in range(3):
-            s = device(i)
-            received(x.at[rows(s)], sem[name + "_r"].at[i])
-            send(
-                x.at[rows(s)],
-                x.at[rows(s)],
-                sem["pass_bases_s"].at[0],
-                sem[name + "_pass_r"].at[0],
-                partner,
-            )
+    for t, i in ((1, 1), (1, 2), (0, 0), (1, 0)):
+        pass_base(t, i)
 
     @pl.loop(0, nb)
     def _(q):
@@ -644,8 +654,7 @@
 
     @pl.loop(0, nb)
     def _(q):
-        received(hop_two.at[rows(q)], sem["two_r"].at[q])
-        received(hop_one.at[1, rows(q)], sem["one_r"].at[nb + q])
+        received(hop_one.at[1, pl.ds(0, 2 * rb)], sem["two_r"].at[q])
 
         def add(at):
             r = at(q * rb)
@@ -798,6 +807,13 @@
     def hand_on(b, s, name, recv_sem, target):
         send(weights.at[b, rows(s)], weights.at[b, rows(s)], sem[name].at[0], recv_sem, target)
 
+    def piece(s, p):
+        return pl.ds(pl.multiple_of(s * rb + p * (rb // 4), rb // 4), rb // 4)
+
+    def hand_on_piece(b, s, p, recv_sem, target):
+        ref = weights.at[b, piece(s, p)]
+        send(ref, ref, sem["pass_s"].at[0], recv_sem, target)
+
     def slot(t, q):
         return sem["out_r"].at[t * nb + q]
 
@@ -844,7 +860,11 @@
     for q in range(nb):
         s = 2 * relative(1 - q % 2, q // 2) + k
         received(weights.at[one, rows(s)], slot(0, q))
-        hand_on(one, s, "pass_s", slot(2, q), 2 * two + k)
+        if q < nb - 1:
+            hand_on(one, s, "pass_s", slot(2, q), 2 * two + k)
+        else:
+            for p in range(4):
+                hand_on_piece(one, s, p, slot(2, q + p), 2 * two + k)
         hand_on(one, s, "pass_s", to_partner, partner)
         s = 2 * relative(q % 2, 1 - q // 2) + k
         received(weights.at[two, rows(s)], slot(1, q))
@@ -855,8 +875,13 @@
 
     for q in range(nb):
         s = 2 * relative(1 - q % 2, 1 - q // 2) + k
-        received(weights.at[chip(0), rows(s)], slot(2, q))
-        hand_on(chip(0), s, "pass_s", to_partner, partner)
+        if q < nb - 1:
+            received(weights.at[chip(0), rows(s)], slot(2, q))
+            hand_on(chip(0), s, "pass_s", to_partner, partner)
+        else:
+            for p in range(4):
+                received(weights.at[chip(0), piece(s, p)], slot(2, q + p))
+                hand_on_piece(chip(0), s, p, to_partner, partner)
 
     finish(0)
 

time: 138 us -> 138 us (level)
  no operation moved by 1% of the time
where the time goes in v4:
time: 138 us; the launch traced here: 137 us
  Pallas kernels  137 us (99%)
    pallas_call x1, Pallas kernels, per_device(): pl.pallas_call(functools.partial(step_kernel, n, m), out_shape=[pltpu.VME...  131 us
    pallas_call x1, Pallas kernels, per_device(): pl.pallas_call(store_kernel, out_shape=shapes, in_specs=[VMEM] * 4, out_s...  5.29 us

profile of v4, /device:TPU:0, one launch (start us, length us, event | category | flops | bytes accessed | tf_op | source)
XLA Modules:
  0.0 137.4 jit_solution(137736861039694296)
XLA Ops:
  0.6 131.4 %shard_map.93 = (bf16[4,1024,1024]{2,1,0:T(8,128)(2,1)S(1)}, f32[4,128,1024]{2,1,0:T(8,128)S(1)}, f32[4,128,1024]{2,1,0:T(8,128)S(1)}, f32[4,128,1024]{2,1,0:T(8,128)S(1)}) custom-call(bf16[4,1024,1024]{2,1,0:T(8,128)(2,1)} %bitcast.1, f32[4,128,1024]{2,1,0:T(8,128)} %master.1, f32[4,128,1024]{2,1,0:T(8,128)} %first.1, f32[4,128,1024]{2,1,0:T(8,128)} %second.1, ...), custom_call_target="tpu_custom_call" | custom-call | tf_op jit(solution)/shard_map/pallas_call | solution.py:965
  132.1 5.3 %shard_map.94 = (bf16[4,1024,1024]{2,1,0:T(8,128)(2,1)}, f32[4,128,1024]{2,1,0:T(8,128)}, f32[4,128,1024]{2,1,0:T(8,128)}, f32[4,128,1024]{2,1,0:T(8,128)}) custom-call(bf16[4,1024,1024]{2,1,0:T(8,128)(2,1)S(1)} %get-tuple-element.8.weights, f32[4,128,1024]{2,1,0:T(8,128)S(1)} %get-tuple-element.9.master, f32[4,128,1024]{2,1,0:T(8,128)S(1)} %get-tuple-element.10.first, ...), custom_call_target="tpu_custom_call" | custom-call | tf_op jit(solution)/shard_map/pallas_call | solution.py:975

commit v5 on v4

--- a/solution.py
+++ b/solution.py
@@ -463,7 +463,7 @@
     c, k = me // 2, lax.rem(me, 2)
     cy, cx = c // 2, lax.rem(c, 2)
     xn, yn = 2 * cy + (1 - cx), 2 * (1 - cy) + cx
-    one, two = (1 - k) * xn + k * yn, k * xn + (1 - k) * yn
+    one, two = k * xn + (1 - k) * yn, (1 - k) * xn + k * yn
     partner = me + 1 - 2 * k
     swapped = (0, 2, 1, 3)
     keep = 1.0 - learning_rate * decay_rate
@@ -790,6 +790,7 @@
         send(back.at[rows(s)], back.at[rows(s)], sem["back_s"].at[0], sem["back_r"].at[0], partner)
 
     back_slab(3, dir_send)
+    send_low(2)
 
     @pl.loop(0, 3)
     def _(i):
@@ -797,7 +798,6 @@
 
         @pl.when(i == 0)
         def _():
-            send_low(2)
             send_low_part(1)
 
         back_slab(i, dir_recv)

time: 138 us -> 137 us (level)
  no operation moved by 1% of the time
where the time goes in v5:
time: 137 us
  Pallas kernels  136 us (99%)
    pallas_call x1, Pallas kernels, per_device(): pl.pallas_call(functools.partial(step_kernel, n, m), out_shape=[pltpu.VME...  131 us
    pallas_call x1, Pallas kernels, per_device(): pl.pallas_call(store_kernel, out_shape=shapes, in_specs=[VMEM] * 4, out_s...  5.29 us

profile of v5, /device:TPU:0, one launch (start us, length us, event | category | flops | bytes accessed | tf_op | source)
XLA Modules:
  0.0 137.0 jit_solution(5094249249850927254)
XLA Ops:
  0.6 131.1 %shard_map.93 = (bf16[4,1024,1024]{2,1,0:T(8,128)(2,1)S(1)}, f32[4,128,1024]{2,1,0:T(8,128)S(1)}, f32[4,128,1024]{2,1,0:T(8,128)S(1)}, f32[4,128,1024]{2,1,0:T(8,128)S(1)}) custom-call(bf16[4,1024,1024]{2,1,0:T(8,128)(2,1)} %bitcast.1, f32[4,128,1024]{2,1,0:T(8,128)} %master.1, f32[4,128,1024]{2,1,0:T(8,128)} %first.1, f32[4,128,1024]{2,1,0:T(8,128)} %second.1, ...), custom_call_target="tpu_custom_call" | custom-call | tf_op jit(solution)/shard_map/pallas_call | solution.py:965
  131.7 5.3 %shard_map.94 = (bf16[4,1024,1024]{2,1,0:T(8,128)(2,1)}, f32[4,128,1024]{2,1,0:T(8,128)}, f32[4,128,1024]{2,1,0:T(8,128)}, f32[4,128,1024]{2,1,0:T(8,128)}) custom-call(bf16[4,1024,1024]{2,1,0:T(8,128)(2,1)S(1)} %get-tuple-element.8.weights, f32[4,128,1024]{2,1,0:T(8,128)S(1)} %get-tuple-element.9.master, f32[4,128,1024]{2,1,0:T(8,128)S(1)} %get-tuple-element.10.first, ...), custom_call_target="tpu_custom_call" | custom-call | tf_op jit(solution)/shard_map/pallas_call | solution.py:975

commit v6 on v5

--- a/solution.py
+++ b/solution.py
@@ -393,24 +393,18 @@
     ("left_s", 1),
     ("left_r", 3),
     ("left_pass_r", 1),
-    ("pass_bases_s", 1),
     ("one_s", 1),
     ("one_r", 4),
-    ("two_s", 1),
     ("two_r", 4),
-    ("turned_s", 1),
     ("turned_r", 1),
     ("rot_s", 1),
     ("rot_r", 3),
-    ("dir_s", 1),
     ("dir_r", 3),
-    ("back_s", 1),
     ("back_r", 1),
     ("low_s", 1),
     ("low_r", 3),
     ("out_s", 1),
     ("pass_s", 1),
-    ("out_r", 15),
     ("out_pass_r", 1),
     ("norm_s", 1),
     ("norm_r", 1),
@@ -560,7 +554,7 @@
         send(
             x.at[rows(s)],
             x.at[rows(s)],
-            sem["pass_bases_s"].at[0],
+            sem["rot_s"].at[0],
             sem[name + "_pass_r"].at[0],
             partner,
         )
@@ -637,7 +631,7 @@
         send(
             acc.at[2, rows(q)],
             hop_two.at[rows(q)],
-            sem["two_s"].at[0],
+            sem["one_s"].at[0],
             sem["two_r"].at[q],
             2 * two + k,
         )
@@ -689,7 +683,7 @@
         send(
             turned.at[rows(s)],
             turned.at[rows(s)],
-            sem["turned_s"].at[0],
+            sem["one_s"].at[0],
             sem["turned_r"].at[0],
             partner,
         )
@@ -778,7 +772,7 @@
     def _(i):
         received(rot_recv.at[i], sem["rot_r"].at[i])
         moments(i, rot_recv)
-        send(dir_send.at[i], dir_recv.at[i], sem["dir_s"].at[0], sem["dir_r"].at[i], device(i))
+        send(dir_send.at[i], dir_recv.at[i], sem["rot_s"].at[0], sem["dir_r"].at[i], device(i))
 
     def back_slab(i, src):
         s = device(i)
@@ -787,7 +781,7 @@
             back[rows(s), at] = lax.dot_general(
                 src[i], right[at, :], (((1,), (1,)), ((), ())), preferred_element_type=f32
             ).astype(bf16)
-        send(back.at[rows(s)], back.at[rows(s)], sem["back_s"].at[0], sem["back_r"].at[0], partner)
+        send(back.at[rows(s)], back.at[rows(s)], sem["out_s"].at[0], sem["back_r"].at[0], partner)
 
     back_slab(3, dir_send)
     send_low(2)
@@ -815,7 +809,9 @@
         send(ref, ref, sem["pass_s"].at[0], recv_sem, target)
 
     def slot(t, q):
-        return sem["out_r"].at[t * nb + q]
+        if t < 2:
+            return sem[("one_r", "two_r")[t]].at[q]
+        return sem[("right_r", "left_r", "pair_r")[q // 3]].at[q % 3]
 
     to_partner = sem["out_pass_r"].at[0]
 
@@ -887,16 +883,11 @@
 
     for ref, name in (
         (pair_recv, "pair_s"),
-        (hop_one, "one_s"),
-        (hop_two, "two_s"),
-        (turned.at[pl.ds(0, half)], "turned_s"),
-        (back.at[pl.ds(0, half)], "back_s"),
-        (rot_send.at[pl.ds(0, 3)], "rot_s"),
-        (dir_send.at[pl.ds(0, 3)], "dir_s"),
+        (acc, "one_s"),
+        (acc.at[pl.ds(0, 3)], "rot_s"),
         (low_send.at[pl.ds(0, 3)], "low_s"),
-        (left.at[pl.ds(0, 6 * rb)], "pass_bases_s"),
         (parts_dp.at[pl.ds(0, n - 1)], "norm_s"),
-        (acc.at[pl.ds(0, 3)], "out_s"),
+        (acc, "out_s"),
         (weights.at[pl.ds(0, 2)], "pass_s"),
     ):
         sent(ref, sem[name].at[0])

time: 137 us -> 137 us (level)
  no operation moved by 1% of the time
where the time goes in v6:
time: 137 us
  Pallas kernels  136 us (99%)
    pallas_call x1, Pallas kernels, per_device(): pl.pallas_call(functools.partial(step_kernel, n, m), out_shape=[pltpu.VME...  131 us
    pallas_call x1, Pallas kernels, per_device(): pl.pallas_call(store_kernel, out_shape=shapes, in_specs=[VMEM] * 4, out_s...  5.29 us

profile of v6, /device:TPU:0, one launch (start us, length us, event | category | flops | bytes accessed | tf_op | source)
XLA Modules:
  0.0 136.9 jit_solution(8340291592538532161)
XLA Ops:
  0.6 130.9 %shard_map.93 = (bf16[4,1024,1024]{2,1,0:T(8,128)(2,1)S(1)}, f32[4,128,1024]{2,1,0:T(8,128)S(1)}, f32[4,128,1024]{2,1,0:T(8,128)S(1)}, f32[4,128,1024]{2,1,0:T(8,128)S(1)}) custom-call(bf16[4,1024,1024]{2,1,0:T(8,128)(2,1)} %bitcast.1, f32[4,128,1024]{2,1,0:T(8,128)} %master.1, f32[4,128,1024]{2,1,0:T(8,128)} %first.1, f32[4,128,1024]{2,1,0:T(8,128)} %second.1, ...), custom_call_target="tpu_custom_call" | custom-call | tf_op jit(solution)/shard_map/pallas_call | solution.py:956
  131.6 5.3 %shard_map.94 = (bf16[4,1024,1024]{2,1,0:T(8,128)(2,1)}, f32[4,128,1024]{2,1,0:T(8,128)}, f32[4,128,1024]{2,1,0:T(8,128)}, f32[4,128,1024]{2,1,0:T(8,128)}) custom-call(bf16[4,1024,1024]{2,1,0:T(8,128)(2,1)S(1)} %get-tuple-element.8.weights, f32[4,128,1024]{2,1,0:T(8,128)S(1)} %get-tuple-element.9.master, f32[4,128,1024]{2,1,0:T(8,128)S(1)} %get-tuple-element.10.first, ...), custom_call_target="tpu_custom_call" | custom-call | tf_op jit(solution)/shard_map/pallas_call | solution.py:966
